TPU v7x, 32 devices: a 4x4x1 block of a 4x4x8 slice. The times are simulated.
32 devices in a mesh: part: 1 (over z), data: 4 (over y), model: 8 (over x, core).
Axes of the slice: x: 4, y: 4, z: 1, core: 2. Of those that a mesh axis runs over, the one named last changes fastest.
The devices are a block of a 4x4x8 slice.
Arguments:
- x: bfloat16 [2, 16, 1024, 2048], P(None, ('part', 'data'), 'model')
- lengths: int32 [2, 16], P(None, ('part', 'data'))
- norm_gain: bfloat16 [2, 2048], P(None, 'data')
- w_in: bfloat16 [2, 2048, 18432], P(None, 'data', 'model')
- w_kv: bfloat16 [2, 2048, 256], P(None, 'data')
- w_out: bfloat16 [2, 10240, 2048], P(None, 'model', 'data')
Outputs:
- output: bfloat16 [2, 16, 1024, 2048], P(None, ('part', 'data'), 'model')
All inputs are finite; a program needn't handle non-finite values.
Results may differ from a plain program's by a relative error of at most 0.014422.
Values are sent between devices in bfloat16 or wider.
A program may use at most 768 MiB of HBM per device.

v0:
```python
import math
import jax
import jax.numpy as jnp
from jax import lax
from jax.sharding import PartitionSpec as P, NamedSharding

NORM_EPS = 1e-6
NEG_BIG = -1e30


def layer_norm(x_act, gain_vec):
    x_f32 = x_act.astype(jnp.float32)
    centered = x_f32 - jnp.mean(x_f32, axis=-1, keepdims=True)
    variance = jnp.mean(centered * centered, axis=-1, keepdims=True)
    return (centered * lax.rsqrt(variance + NORM_EPS) * gain_vec.astype(jnp.float32)).astype(jnp.bfloat16)


def attention(q_heads, k_all, v_all, seq_lens, q_offset):
    q_len = q_heads.shape[1]
    k_len = k_all.shape[1]
    head_dim = k_all.shape[2]
    scores = jnp.einsum("bqhc,bkc->bhqk", q_heads, k_all, preferred_element_type=jnp.float32) * (1.0 / math.sqrt(head_dim))
    q_pos = q_offset + lax.broadcasted_iota(jnp.int32, (q_len, 1), 0)
    k_pos = lax.broadcasted_iota(jnp.int32, (1, k_len), 1)
    allowed = (k_pos <= q_pos)[None, None] & (k_pos[None, None] < seq_lens[:, None, None, None])
    scores = jnp.where(allowed, scores, NEG_BIG)
    attn_probs = jax.nn.softmax(scores, axis=-1).astype(jnp.bfloat16)
    return jnp.einsum("bhqk,bkc->bqhc", attn_probs, v_all, preferred_element_type=jnp.float32).astype(jnp.bfloat16)


def layer_block(x_loc, seq_lens, gain_full, w_in3, w_kv_full, w_out3, n_model):
    n_seqs, t_loc, d_model = x_loc.shape
    head_dim = w_kv_full.shape[1] // 2
    ff_head = (w_in3.shape[2] - head_dim) // 2
    h_loc = layer_norm(x_loc, gain_full)
    h_all = lax.all_gather(h_loc, "model", axis=1, tiled=True)
    projected = jnp.einsum("btd,dhc->bthc", h_all, w_in3, preferred_element_type=jnp.float32).astype(jnp.bfloat16)
    kv_act = jnp.einsum("btd,dc->btc", h_all, w_kv_full, preferred_element_type=jnp.float32).astype(jnp.bfloat16)
    attn_out = attention(projected[..., :head_dim], kv_act[..., :head_dim], kv_act[..., head_dim:], seq_lens, 0)
    gate_act = projected[..., head_dim:head_dim + ff_head]
    up_act = projected[..., head_dim + ff_head:]
    mlp_out = (jax.nn.silu(gate_act.astype(jnp.float32)) * up_act.astype(jnp.float32)).astype(jnp.bfloat16)
    joined = jnp.concatenate([attn_out, mlp_out], axis=-1)
    group_sum = jnp.einsum("bthc,hcd->btd", joined, w_out3, preferred_element_type=jnp.float32).astype(jnp.bfloat16)
    received = lax.all_to_all(group_sum.reshape(n_seqs, n_model, t_loc, d_model), "model", 1, 1, tiled=True)
    z_sum = jnp.sum(received.astype(jnp.float32), axis=1)
    return (x_loc.astype(jnp.float32) + z_sum).astype(jnp.bfloat16)


def solution(mesh):
    n_model = mesh.shape["model"]
    act_spec = P(None, ("part", "data"), "model", None)

    def local_fn(x_blk, len_blk, gain_blk, w_in_blk, w_kv_blk, w_out_blk):
        head_dim = w_kv_blk.shape[2] // 2
        hidden = [x_blk[micro_idx] for micro_idx in range(x_blk.shape[0])]
        for layer_idx in range(gain_blk.shape[0]):
            gain_full = lax.all_gather(gain_blk[layer_idx], "data", axis=0, tiled=True)
            w_in_loc = lax.all_gather(w_in_blk[layer_idx], "data", axis=0, tiled=True)
            w_kv_full = lax.all_gather(w_kv_blk[layer_idx], "data", axis=0, tiled=True)
            w_out_loc = lax.all_gather(w_out_blk[layer_idx], "data", axis=1, tiled=True)
            d_model, in_loc = w_in_loc.shape
            out_loc = w_out_loc.shape[0]
            ff_loc = in_loc - out_loc
            heads_loc = (out_loc - ff_loc) // head_dim
            w_in3 = w_in_loc.reshape(d_model, heads_loc, in_loc // heads_loc)
            w_out3 = w_out_loc.reshape(heads_loc, out_loc // heads_loc, d_model)
            for micro_idx in range(len(hidden)):
                hidden[micro_idx] = layer_block(hidden[micro_idx], len_blk[micro_idx], gain_full, w_in3, w_kv_full, w_out3, n_model)
        return jnp.stack(hidden)

    return jax.shard_map(
        local_fn,
        mesh=mesh,
        in_specs=(act_spec, P(None, ("part", "data")), P(None, "data"), P(None, "data", "model"), P(None, "data", None), P(None, "model", "data")),
        out_specs=act_spec,
        check_vma=False,
    )
```

profile of v0, /device:TPU:97, one launch (start us, length us, event | category | flops | bytes accessed | tf_op | source)
XLA Modules:
  0.0 1443.0 jit_solution(1986033951437818314)
XLA Ops:
  12.9 12.0 all-gather
  48.1 71.4 %all-gather.23.cloned.1.call-done = bf16[4,1024,2048]{2,1,0:T(8,128)(2,1)} async-done(((bf16[4,128,2048]{2,1,0:T(8,128)(2,1)}), bf16[4,1024,2048]{2,1,0:T(8,128)(2,1)}) %all-gather.23.cloned.1.call-update) | async-done | bytes 16777232 | tf_op jit(solution)/shard_map/all_gather | solution.py:36
  119.6 10.5 convolution_convert_fusion.5
  130.1 80.7 %all-gather.29.cloned.1.call-done = bf16[1,2048,2304]{1,2,0:T(8,128)(2,1)} async-done(((bf16[1,512,2304]{1,2,0:T(8,128)(2,1)}), bf16[1,2048,2304]{1,2,0:T(8,128)(2,1)}) %all-gather.29.cloned.1.call-update) | async-done | bytes 9437200 | tf_op jit(solution)/shard_map/all_gather | solution.py:59
  210.8 46.4 %convolution_convert_fusion.1 = bf16[4,1024,2,1152]{3,1,2,0:T(8,128)(2,1)} fusion(bf16[2048,2,1152,1]{0,2,1,3:T(8,128)(2,1)} %bitcast.260, bf16[4,1024,2048]{2,1,0:T(8,128)(2,1)} %all-gather.23.cloned.1.call-done), kind=kOutput, calls=%fused_computation.29 | convolution fusion | flops 38664142848 | bytes 45088768 | tf_op jit(solution)/shard_map/btd,dhc->bthc/dot_general | solution.py:37
  257.2 18.0 %fusion.153 = (f32[4,2,1024]{2,1,0:T(2,128)S(1)}, f32[4,2,1024,1024]{2,3,1,0:T(8,128)}) fusion(pred[4,1024,1024]{1,2,0:T(8,128)(4,1)} %get-tuple-element.24, bf16[4,1024,2,1152]{3,1,2,0:T(8,128)(2,1)} %convolution_convert_fusion.1, bf16[4,1024,256]{2,1,0:T(8,128)(2,1)S(1)} %convolution_convert_fusion.5), kind=kOutput, calls=%fused_computation.203 | convolution fusion | flops 2181039104 | bytes 40927232 | tf_op jit(solution)/shard_map/sub | solution.py:27
  275.3 15.3 %convert_bitcast_fusion.3 = bf16[4,1024,2,128]{3,1,2,0:T(8,128)(2,1)} fusion(f32[4,2,1024,1024]{2,3,1,0:T(8,128)} %get-tuple-element.36, f32[4,2,1024]{2,1,0:T(2,128)S(1)} %get-tuple-element.35, bf16[4,1024,256]{2,1,0:T(8,128)(2,1)S(1)} %convolution_convert_fusion.5), kind=kOutput, calls=%fused_computation.143 | convolution fusion | flops 2165309440 | bytes 36732928 | tf_op jit(solution)/shard_map/bhqk,bkc->bqhc/dot_general | solution.py:28
  290.6 11.3 fusion.37
  301.9 25.5 %bitcast_convert_fusion.1 = bf16[4,1024,2048]{2,1,0:T(8,128)(2,1)S(1)} fusion(bf16[2,640,2048,1]{2,1,0,3:T(8,128)(2,1)} %bitcast.264, bf16[4,1024,2,512]{3,1,2,0:T(8,128)(2,1)} %fusion.37, bf16[4,1024,2,128]{3,1,2,0:T(8,128)(2,1)S(1)} %copy-done.15), kind=kOutput, calls=%fused_computation.6 | convolution fusion | flops 21504196608 | bytes 32505856 | tf_op jit(solution)/shard_map/bthc,hcd->btd/dot_general | solution.py:44
  341.2 23.4 %all-gather.19.cloned.1.call-done = bf16[4,1024,2048]{2,1,0:T(8,128)(2,1)} async-done(((bf16[4,128,2048]{2,1,0:T(8,128)(2,1)}), bf16[4,1024,2048]{2,1,0:T(8,128)(2,1)}) %all-gather.19.cloned.1.call-update) | async-done | bytes 16777232 | tf_op jit(solution)/shard_map/all_gather | solution.py:36
  364.6 46.4 %convolution_convert_fusion.3 = bf16[4,1024,2,1152]{3,1,2,0:T(8,128)(2,1)} fusion(bf16[2048,2,1152,1]{0,2,1,3:T(8,128)(2,1)} %bitcast.261, bf16[4,1024,2048]{2,1,0:T(8,128)(2,1)} %all-gather.19.cloned.1.call-done), kind=kOutput, calls=%fused_computation.31 | convolution fusion | flops 38664142848 | bytes 45088768 | tf_op jit(solution)/shard_map/btd,dhc->bthc/dot_general | solution.py:37
  419.4 17.9 %fusion.148 = (f32[4,2,1024]{2,1,0:T(2,128)S(1)}, f32[4,2,1024,1024]{2,3,1,0:T(8,128)}) fusion(pred[4,1024,1024]{1,2,0:T(8,128)(4,1)} %get-tuple-element.23, bf16[4,1024,2,1152]{3,1,2,0:T(8,128)(2,1)} %convolution_convert_fusion.3, bf16[4,1024,256]{2,1,0:T(8,128)(2,1)S(1)} %convolution_convert_fusion.7), kind=kOutput, calls=%fused_computation.202 | convolution fusion | flops 2181039104 | bytes 40927232 | tf_op jit(solution)/shard_map/sub | solution.py:27
  437.2 15.7 %convert_bitcast_fusion.5 = bf16[4,1024,2,128]{3,1,2,0:T(8,128)(2,1)} fusion(f32[4,2,1024,1024]{2,3,1,0:T(8,128)} %get-tuple-element.34, f32[4,2,1024]{2,1,0:T(2,128)S(1)} %get-tuple-element.33, bf16[4,1024,256]{2,1,0:T(8,128)(2,1)S(1)} %convolution_convert_fusion.7), kind=kOutput, calls=%fused_computation.145 | convolution fusion | flops 2165309440 | bytes 36732928 | tf_op jit(solution)/shard_map/bhqk,bkc->bqhc/dot_general | solution.py:28
  452.9 11.3 fusion.39
  464.2 25.6 %bitcast_convert_fusion.3 = bf16[4,1024,2048]{2,1,0:T(8,128)(2,1)S(1)} fusion(bf16[2,640,2048,1]{2,1,0,3:T(8,128)(2,1)} %bitcast.265, bf16[4,1024,2,512]{3,1,2,0:T(8,128)(2,1)} %fusion.39, bf16[4,1024,2,128]{3,1,2,0:T(8,128)(2,1)S(1)} %copy-done.17), kind=kOutput, calls=%fused_computation.10 | convolution fusion | flops 21504196608 | bytes 32505856 | tf_op jit(solution)/shard_map/bthc,hcd->btd/dot_general | solution.py:44
  496.9 33.7 %all-to-all-done.2 = bf16[4,8,128,2048]{3,2,0,1:T(8,128)(2,1)} async-done(((bf16[4,8,128,2048]{3,2,0,1:T(8,128)(2,1)}), bf16[4,8,128,2048]{3,2,0,1:T(8,128)(2,1)}, u32[]{:S(2)}, u32[]{:S(2)}) %all-to-all-start.2) | async-done | bytes 16777248 | tf_op jit(solution)/shard_map/all_to_all | solution.py:45
  557.5 162.8 %all-to-all-done = bf16[4,8,128,2048]{3,2,0,1:T(8,128)(2,1)} async-done(((bf16[4,8,128,2048]{3,2,0,1:T(8,128)(2,1)}), bf16[4,8,128,2048]{3,2,0,1:T(8,128)(2,1)}, u32[]{:S(2)}, u32[]{:S(2)}) %all-to-all-start) | async-done | bytes 16777248 | tf_op jit(solution)/shard_map/all_to_all | solution.py:45
  739.6 78.8 %all-gather.25.cloned.1.call-done = bf16[4,1024,2048]{2,1,0:T(8,128)(2,1)} async-done(((bf16[4,128,2048]{2,1,0:T(8,128)(2,1)}), bf16[4,1024,2048]{2,1,0:T(8,128)(2,1)}) %all-gather.25.cloned.1.call-update) | async-done | bytes 16777232 | tf_op jit(solution)/shard_map/all_gather | solution.py:36
  828.9 80.7 %all-gather.35.cloned.1.call-done = bf16[1,2048,2304]{1,2,0:T(8,128)(2,1)} async-done(((bf16[1,512,2304]{1,2,0:T(8,128)(2,1)}), bf16[1,2048,2304]{1,2,0:T(8,128)(2,1)}) %all-gather.35.cloned.1.call-update) | async-done | bytes 9437200 | tf_op jit(solution)/shard_map/all_gather | solution.py:59
  909.6 46.7 %convolution_convert_fusion = bf16[4,1024,2,1152]{3,1,2,0:T(8,128)(2,1)} fusion(bf16[2048,2,1152,1]{0,2,1,3:T(8,128)(2,1)} %bitcast.262, bf16[4,1024,2048]{2,1,0:T(8,128)(2,1)} %all-gather.25.cloned.1.call-done), kind=kOutput, calls=%fused_computation.28 | convolution fusion | flops 38664142848 | bytes 45088768 | tf_op jit(solution)/shard_map/btd,dhc->bthc/dot_general | solution.py:37
  956.3 17.9 %fusion.163 = (f32[4,2,1024]{2,1,0:T(2,128)S(1)}, f32[4,2,1024,1024]{2,3,1,0:T(8,128)}) fusion(pred[4,1024,1024]{1,2,0:T(8,128)(4,1)} %get-tuple-element.24, bf16[4,1024,2,1152]{3,1,2,0:T(8,128)(2,1)} %convolution_convert_fusion, bf16[4,1024,256]{2,1,0:T(8,128)(2,1)S(1)} %convolution_convert_fusion.4), kind=kOutput, calls=%fused_computation.205 | convolution fusion | flops 2181039104 | bytes 40927232 | tf_op jit(solution)/shard_map/sub | solution.py:27
  974.1 15.4 %convert_bitcast_fusion.2 = bf16[4,1024,2,128]{3,1,2,0:T(8,128)(2,1)} fusion(f32[4,2,1024,1024]{2,3,1,0:T(8,128)} %get-tuple-element.40, f32[4,2,1024]{2,1,0:T(2,128)S(1)} %get-tuple-element.39, bf16[4,1024,256]{2,1,0:T(8,128)(2,1)S(1)} %convolution_convert_fusion.4), kind=kOutput, calls=%fused_computation.142 | convolution fusion | flops 2165309440 | bytes 36732928 | tf_op jit(solution)/shard_map/bhqk,bkc->bqhc/dot_general | solution.py:28
  989.5 11.8 fusion.36
  1001.3 25.5 %bitcast_convert_fusion = bf16[4,1024,2048]{2,1,0:T(8,128)(2,1)S(1)} fusion(bf16[2,640,2048,1]{2,1,0,3:T(8,128)(2,1)} %bitcast.266, bf16[4,1024,2,512]{3,1,2,0:T(8,128)(2,1)} %fusion.36, bf16[4,1024,2,128]{3,1,2,0:T(8,128)(2,1)S(1)} %copy-done.16), kind=kOutput, calls=%fused_computation.4 | convolution fusion | flops 21504196608 | bytes 32505856 | tf_op jit(solution)/shard_map/bthc,hcd->btd/dot_general | solution.py:44
  1040.5 22.1 %all-gather.21.cloned.1.call-done = bf16[4,1024,2048]{2,1,0:T(8,128)(2,1)} async-done(((bf16[4,128,2048]{2,1,0:T(8,128)(2,1)}), bf16[4,1024,2048]{2,1,0:T(8,128)(2,1)}) %all-gather.21.cloned.1.call-update) | async-done | bytes 16777232 | tf_op jit(solution)/shard_map/all_gather | solution.py:36
  1062.7 46.4 %convolution_convert_fusion.2 = bf16[4,1024,2,1152]{3,1,2,0:T(8,128)(2,1)} fusion(bf16[2048,2,1152,1]{0,2,1,3:T(8,128)(2,1)} %bitcast.263, bf16[4,1024,2048]{2,1,0:T(8,128)(2,1)} %all-gather.21.cloned.1.call-done), kind=kOutput, calls=%fused_computation.30 | convolution fusion | flops 38664142848 | bytes 45088768 | tf_op jit(solution)/shard_map/btd,dhc->bthc/dot_general | solution.py:37
  1117.5 17.9 %fusion.158 = (f32[4,2,1024]{2,1,0:T(2,128)S(1)}, f32[4,2,1024,1024]{2,3,1,0:T(8,128)}) fusion(pred[4,1024,1024]{1,2,0:T(8,128)(4,1)} %get-tuple-element.23, bf16[4,1024,2,1152]{3,1,2,0:T(8,128)(2,1)} %convolution_convert_fusion.2, bf16[4,1024,256]{2,1,0:T(8,128)(2,1)S(1)} %convolution_convert_fusion.6), kind=kOutput, calls=%fused_computation.204 | convolution fusion | flops 2181039104 | bytes 40927232 | tf_op jit(solution)/shard_map/sub | solution.py:27
  1135.3 15.5 %convert_bitcast_fusion.4 = bf16[4,1024,2,128]{3,1,2,0:T(8,128)(2,1)} fusion(f32[4,2,1024,1024]{2,3,1,0:T(8,128)} %get-tuple-element.38, f32[4,2,1024]{2,1,0:T(2,128)S(1)} %get-tuple-element.37, bf16[4,1024,256]{2,1,0:T(8,128)(2,1)S(1)} %convolution_convert_fusion.6), kind=kOutput, calls=%fused_computation.144 | convolution fusion | flops 2165309440 | bytes 36732928 | tf_op jit(solution)/shard_map/bhqk,bkc->bqhc/dot_general | solution.py:28
  1150.8 11.3 fusion.38
  1162.1 25.6 %bitcast_convert_fusion.2 = bf16[4,1024,2048]{2,1,0:T(8,128)(2,1)S(1)} fusion(bf16[2,640,2048,1]{2,1,0,3:T(8,128)(2,1)} %bitcast.267, bf16[4,1024,2,512]{3,1,2,0:T(8,128)(2,1)} %fusion.38, bf16[4,1024,2,128]{3,1,2,0:T(8,128)(2,1)S(1)} %copy-done.18), kind=kOutput, calls=%fused_computation.8 | convolution fusion | flops 21504196608 | bytes 32505856 | tf_op jit(solution)/shard_map/bthc,hcd->btd/dot_general | solution.py:44
  1194.8 34.7 %all-to-all-done.3 = bf16[4,8,128,2048]{3,2,0,1:T(8,128)(2,1)} async-done(((bf16[4,8,128,2048]{3,2,0,1:T(8,128)(2,1)}), bf16[4,8,128,2048]{3,2,0,1:T(8,128)(2,1)}, u32[]{:S(2)}, u32[]{:S(2)}) %all-to-all-start.3) | async-done | bytes 16777248 | tf_op jit(solution)/shard_map/all_to_all | solution.py:45
  1245.0 174.3 %all-to-all-done.1 = bf16[4,8,128,2048]{3,2,0,1:T(8,128)(2,1)} async-done(((bf16[4,8,128,2048]{3,2,0,1:T(8,128)(2,1)}), bf16[4,8,128,2048]{3,2,0,1:T(8,128)(2,1)}, u32[]{:S(2)}, u32[]{:S(2)}) %all-to-all-start.1) | async-done | bytes 16777248 | tf_op jit(solution)/shard_map/all_to_all | solution.py:45
  (106 shorter events, 176.3 us)
Async XLA Ops:
  6.5 41.6 %all-gather.27.cloned.1.call-start = ((), (), s32[]{:S(2)}) async-start(), calls=%async_computation.8 | async-start | bytes 1310720 | tf_op jit(solution)/shard_map/all_gather | solution.py:60
  8.5 111.1 %all-gather.23.cloned.1.call-start = ((), (), s32[]{:S(2)}) async-start(), calls=%async_computation.6 | async-start | bytes 18874368 | tf_op jit(solution)/shard_map/all_gather | solution.py:36
  8.6 19.4 %copy-start = (bf16[2,4,128,2048]{3,2,1,0:T(8,128)(2,1)S(1)}, bf16[2,4,128,2048]{3,2,1,0:T(8,128)(2,1)}, u32[]{:S(2)}) copy-start(bf16[2,4,128,2048]{3,2,1,0:T(8,128)(2,1)} %param.6) | copy-start | bytes 12582916
  30.8 180.0 %all-gather.29.cloned.1.call-start = ((), (), s32[]{:S(2)}) async-start(), calls=%async_computation.9 | async-start | bytes 11796480 | tf_op jit(solution)/shard_map/all_gather | solution.py:59
  35.0 7.0 copy-start.10
  37.5 264.4 %all-gather.31.cloned.1.call-start = ((), (), s32[]{:S(2)}) async-start(), calls=%async_computation.10 | async-start | bytes 6553600 | tf_op jit(solution)/shard_map/all_gather | solution.py:61
  41.0 323.5 %all-gather.19.cloned.1.call-start = ((), (), s32[]{:S(2)}) async-start(), calls=%async_computation.4 | async-start | bytes 18874368 | tf_op jit(solution)/shard_map/all_gather | solution.py:36
  290.6 11.3 copy-start.15
  334.6 196.0 %all-to-all-start.2 = ((bf16[4,8,128,2048]{3,2,0,1:T(8,128)(2,1)}), bf16[4,8,128,2048]{3,2,0,1:T(8,128)(2,1)}, u32[]{:S(2)}, u32[]{:S(2)}) async-start(bf16[4,8,128,2048]{3,2,0,1:T(8,128)(2,1)} %copy.29), calls=%async_computation.2 | async-start | bytes 33554432 | tf_op jit(solution)/shard_map/all_to_all | solution.py:45
  341.2 69.8 %copy-start.13 = (bf16[1,2048,256]{2,1,0:T(8,128)(2,1)S(1)}, bf16[1,2048,256]{2,1,0:T(8,128)(2,1)}, u32[]{:S(2)}) copy-start(bf16[1,2048,256]{2,1,0:T(8,128)(2,1)} %all-gather.27.cloned.1.call-done) | copy-start | bytes 3145732
  452.9 11.3 copy-start.17
  496.9 40.6 %copy-start.9 = (bf16[1,512]{1,0:T(2,128)(2,1)S(1)}, bf16[1,512]{1,0:T(2,128)(2,1)}, u32[]{:S(2)}) copy-start(bf16[1,512]{1,0:T(2,128)(2,1)} %get-tuple-element.29) | copy-start | bytes 3076
  530.6 189.8 %all-to-all-start = ((bf16[4,8,128,2048]{3,2,0,1:T(8,128)(2,1)}), bf16[4,8,128,2048]{3,2,0,1:T(8,128)(2,1)}, u32[]{:S(2)}, u32[]{:S(2)}) async-start(bf16[4,8,128,2048]{3,2,0,1:T(8,128)(2,1)} %copy.18), calls=%async_computation | async-start | bytes 33554432 | tf_op jit(solution)/shard_map/all_to_all | solution.py:45
  536.8 202.7 %all-gather.33.cloned.1.call-start = ((), (), s32[]{:S(2)}) async-start(), calls=%async_computation.11 | async-start | bytes 1310720 | tf_op jit(solution)/shard_map/all_gather | solution.py:60
  537.4 280.9 %all-gather.25.cloned.1.call-start = ((), (), s32[]{:S(2)}) async-start(), calls=%async_computation.7 | async-start | bytes 18874368 | tf_op jit(solution)/shard_map/all_gather | solution.py:36
  720.3 8.9 copy-start.1
  720.3 8.9 copy-start.3
  731.2 4.3 copy-start.8
  735.5 174.2 %all-gather.35.cloned.1.call-start = ((), (), s32[]{:S(2)}) async-start(), calls=%async_computation.12 | async-start | bytes 11796480 | tf_op jit(solution)/shard_map/all_gather | solution.py:59
  738.1 263.2 %all-gather.37.cloned.1.call-start = ((), (), s32[]{:S(2)}) async-start(), calls=%async_computation.13 | async-start | bytes 6553600 | tf_op jit(solution)/shard_map/all_gather | solution.py:61
  738.9 323.8 %all-gather.21.cloned.1.call-start = ((), (), s32[]{:S(2)}) async-start(), calls=%async_computation.5 | async-start | bytes 18874368 | tf_op jit(solution)/shard_map/all_gather | solution.py:36
  989.5 11.8 copy-start.16
  1034.0 195.5 %all-to-all-start.3 = ((bf16[4,8,128,2048]{3,2,0,1:T(8,128)(2,1)}), bf16[4,8,128,2048]{3,2,0,1:T(8,128)(2,1)}, u32[]{:S(2)}, u32[]{:S(2)}) async-start(bf16[4,8,128,2048]{3,2,0,1:T(8,128)(2,1)} %copy.34), calls=%async_computation.3 | async-start | bytes 33554432 | tf_op jit(solution)/shard_map/all_to_all | solution.py:45
  1040.5 68.6 %copy-start.14 = (bf16[1,2048,256]{2,1,0:T(8,128)(2,1)S(1)}, bf16[1,2048,256]{2,1,0:T(8,128)(2,1)}, u32[]{:S(2)}) copy-start(bf16[1,2048,256]{2,1,0:T(8,128)(2,1)} %all-gather.33.cloned.1.call-done) | copy-start | bytes 3145732
  1150.8 11.3 copy-start.18
  1229.5 189.8 %all-to-all-start.1 = ((bf16[4,8,128,2048]{3,2,0,1:T(8,128)(2,1)}), bf16[4,8,128,2048]{3,2,0,1:T(8,128)(2,1)}, u32[]{:S(2)}, u32[]{:S(2)}) async-start(bf16[4,8,128,2048]{3,2,0,1:T(8,128)(2,1)} %copy.24), calls=%async_computation.1 | async-start | bytes 33554432 | tf_op jit(solution)/shard_map/all_to_all | solution.py:45
  1419.3 9.0 copy-start.2
  1419.3 9.0 copy-start.4
  1419.3 9.6 copy-start.6
  1419.3 10.7 copy-start.7
  1419.3 11.9 copy-start.11
  1434.0 2.0 copy-start.12
  (1 other events, 2.0 us)
Sparse Core Ops, SparseCore 0:
  8.9 23.2 all-gather.26
  33.8 85.7 all-gather.22
  121.2 89.6 all-gather.28
  212.2 55.2 all-gather.30
  269.0 95.5 all-gather.18
  538.9 20.6 all-gather.32
  735.6 82.7 all-gather.24
  819.9 89.6 all-gather.34
  911.2 55.3 all-gather.36
  968.0 94.6 all-gather.20
where the time goes:
time: 1450 us; the launch traced here: 1440 us
  waiting for transfers between devices  765 us (53%)
  matrix products  459 us (32%)
  other arithmetic  105 us (7%)
  local copies, waits for them, and re-layouts  49.9 us (3%)
  starting transfers between devices  26.7 us (2%)
  blocking collectives  22.5 us (2%)
    all_to_all x4, waiting for transfers between devices, layer_block(): lax.all_to_all(group_sum.reshape(n_seqs, n_model, t_loc, d_model), 'model...  406 us
    all_gather x4, waiting for transfers between devices, layer_block(): h_all = lax.all_gather(h_loc, 'model', axis=1, tiled=True)  196 us
    dot_general x4, matrix products, layer_block(): jnp.einsum('btd,dhc->bthc', h_all, w_in3, preferred_element_type=jnp.floa...  186 us
    all_gather x2, waiting for transfers between devices, local_fn(): w_in_loc = lax.all_gather(w_in_blk[layer_idx], 'data', axis=0, tiled=True)  161 us
    dot_general x4, matrix products, layer_block(): jnp.einsum('bthc,hcd->btd', joined, w_out3, preferred_element_type=jnp.fl...  102 us
    sub x4, matrix products, attention(): attn_probs = jax.nn.softmax(scores, axis=-1).astype(jnp.bfloat16)  71.6 us
    dot_general x4, matrix products, attention(): jnp.einsum('bhqk,bkc->bqhc', attn_probs, v_all, preferred_element_type=jn...  61.8 us
    convert_element_type x4, other arithmetic, layer_block(): (jax.nn.silu(gate_act.astype(jnp.float32)) * up_act.astype(jnp.float32))....  45.7 us
  transfers between devices with their start and end apart: 14, of which 10 were waited for; matrix products, arithmetic and copies ran while one was open for 41% of the time, Pallas kernels for 0%

commit v1 on v0

v1 whole, which is shorter than its diff:
```python
import math
import jax
import jax.numpy as jnp
from jax import lax
from jax.sharding import PartitionSpec as P

NORM_EPS = 1e-6
NEG_BIG = -1e30


def layer_norm(x_act, gain_vec):
    x_f32 = x_act.astype(jnp.float32)
    centered = x_f32 - jnp.mean(x_f32, axis=-1, keepdims=True)
    variance = jnp.mean(centered * centered, axis=-1, keepdims=True)
    return (centered * lax.rsqrt(variance + NORM_EPS) * gain_vec.astype(jnp.float32)).astype(jnp.bfloat16)


def attention(q_heads, k_all, v_all, seq_lens, q_offset):
    q_len = q_heads.shape[2]
    k_len = k_all.shape[1]
    head_dim = k_all.shape[2]
    scores = jnp.einsum("gbqc,bkc->bgqk", q_heads, k_all, preferred_element_type=jnp.float32) * (1.0 / math.sqrt(head_dim))
    q_pos = q_offset + lax.broadcasted_iota(jnp.int32, (q_len, 1), 0)
    k_pos = lax.broadcasted_iota(jnp.int32, (1, k_len), 1)
    allowed = (k_pos <= q_pos)[None, None] & (k_pos[None, None] < seq_lens[:, None, None, None])
    scores = jnp.where(allowed, scores, NEG_BIG)
    probs = jax.nn.softmax(scores, axis=-1).astype(jnp.bfloat16)
    return jnp.einsum("bgqk,bkc->gbqc", probs, v_all, preferred_element_type=jnp.float32).astype(jnp.bfloat16)


def solution(mesh):
    n_model = mesh.shape["model"]
    n_data = mesh.shape["data"]
    act_spec = P(None, ("part", "data"), "model", None)
    ring = ("model", "data")
    out_splits = (1, 2)

    def gather(arr, axes, axis):
        return lax.all_gather(arr, axes, axis=axis, tiled=True)

    def layers_fn(x_blk, len_blk, gain_blk, w_in_blk, w_kv_blk, w_out_blk):
        n_layers, feat, in_loc = w_in_blk.shape
        head_dim = w_kv_blk.shape[2] // 2
        out_loc = w_out_blk.shape[1]
        heads_loc = (out_loc - (in_loc - out_loc)) // head_dim
        unit_in = in_loc // heads_loc
        unit_out = out_loc // heads_loc
        ff_head = unit_out - head_dim
        n_micro, n_seqs, t_loc, d_model = x_blk.shape
        n_batch = n_micro * n_seqs
        rows = n_batch * t_loc
        lens = len_blk.reshape(n_batch)
        q_offset = lax.axis_index("model") * t_loc

        small = jnp.concatenate([w_kv_blk, jnp.broadcast_to(gain_blk[..., None], gain_blk.shape + (head_dim,))], axis=2)
        small = gather(small, "data", 1)
        hidden = x_blk.reshape(rows, d_model)
        for layer in range(n_layers):
            w_ins = []
            for c in range(heads_loc):
                piece = w_in_blk[layer, :, c * unit_in:(c + 1) * unit_in]
                piece = gather(piece, ring, 0)
                w_ins.append(piece.reshape(n_model, d_model, unit_in))
            splits = out_splits[layer]
            col = feat // splits
            w_outs = []
            for c in range(splits):
                piece = w_out_blk[layer, :, c * col:(c + 1) * col]
                piece = gather(piece, ring, 0)
                w_outs.append(piece.reshape(n_model, n_data, out_loc, col))

            h = layer_norm(hidden, small[layer, :, 2 * head_dim])
            kv = jnp.dot(h, small[layer, :, :2 * head_dim], preferred_element_type=jnp.float32).astype(jnp.bfloat16)
            kv = gather(kv.reshape(n_batch, t_loc, 2 * head_dim), "model", 1)
            joined = []
            for c in range(heads_loc):
                proj = jnp.einsum("td,gdf->gtf", h, w_ins[c], preferred_element_type=jnp.float32).astype(jnp.bfloat16)
                gate = proj[..., head_dim:head_dim + ff_head].astype(jnp.float32)
                up = proj[..., head_dim + ff_head:].astype(jnp.float32)
                m = (jax.nn.silu(gate) * up).astype(jnp.bfloat16)
                q = proj[..., :head_dim].reshape(n_model, n_batch, t_loc, head_dim)
                o = attention(q, kv[..., :head_dim], kv[..., head_dim:], lens, q_offset)
                joined += [o.reshape(n_model, rows, head_dim), m]
            joined = jnp.concatenate(joined, axis=-1)
            zs = []
            for c in range(splits):
                z = jnp.zeros((n_data, rows, col), jnp.float32)
                for g in range(n_model):
                    zg = jnp.einsum("tr,yrc->ytc", joined[g], w_outs[c][g], preferred_element_type=jnp.float32)
                    z = z + zg.astype(jnp.bfloat16).astype(jnp.float32)
                zs.append(z)
            z = jnp.concatenate(zs, axis=-1).transpose(1, 0, 2).reshape(rows, d_model)
            hidden = (hidden.astype(jnp.float32) + z).astype(jnp.bfloat16)
        return hidden.reshape(x_blk.shape)

    return jax.shard_map(
        layers_fn,
        mesh=mesh,
        in_specs=(act_spec, P(None, ("part", "data")), P(None, "data"), P(None, "data", "model"), P(None, "data", None), P(None, "model", "data")),
        out_specs=act_spec,
        check_vma=False,
    )
```

time: 1450 us -> 1170 us (0.81)
  waiting for transfers between devices: 765 us -> 391 us
  local copies, waits for them, and re-layouts: 49.9 us -> 166 us
  matrix products: 459 us -> 498 us
  starting transfers between devices: 26.7 us -> 0.74 us
  blocking collectives: 22.5 us -> 0 us
  other arithmetic: 105 us -> 89.7 us
    all_to_all x4 -> x0, waiting for transfers between devices: 406 us -> none  [layer_block(): lax.all_to_all(group_sum.reshape(n_seqs, n_model, t_loc, d_model), 'model...]
    slice x4 -> x10, local copies, waits for them, and re-layouts: 10.8 us -> 71.5 us  [the longest x3 56.9 us: layers_fn(): w_outs[c][g]]
    dot_general x16 -> x34, matrix products: 388 us -> 436 us  [the longest x4 180 us: layers_fn(): jnp.einsum('td,gdf->gtf', h, w_ins[c], preferred_element_type=jnp.float32)]
    reduce_sum x4 -> x0, other arithmetic: 36.5 us -> none  [layer_block(): z_sum = jnp.sum(received.astype(jnp.float32), axis=1)]
    all_gather x10, waiting for transfers between devices: 357 us -> 388 us  [gather(): return lax.all_gather(arr, axes, axis=axis, tiled=True)]
    convert_element_type x0 -> x7, local copies, waits for them, and re-layouts: none -> 30.2 us  [the longest x2 20.9 us: layers_fn(): hidden = (hidden.astype(jnp.float32) + z).astype(jnp.bfloat16)]
    all_to_all x4 -> x0, starting transfers between devices: 25.7 us -> none  [layer_block(): lax.all_to_all(group_sum.reshape(n_seqs, n_model, t_loc, d_model), 'model...]
    all_gather x2 -> x0, blocking collectives: 22.5 us -> none  [local_fn(): gain_full = lax.all_gather(gain_blk[layer_idx], 'data', axis=0, tiled=True)]
  transfers between devices with their start and end apart: 14 -> 10, of which waited for: 10 -> 7; matrix products, arithmetic and copies ran while one was open for 41% -> 46% of each run, Pallas kernels for 0% -> 0%
where the time goes in v1:
time: 1170 us; the launch traced here: 1160 us
  matrix products  498 us (43%)
  waiting for transfers between devices  391 us (33%)
  local copies, waits for them, and re-layouts  166 us (14%)
  other arithmetic  89.7 us (8%)
  between operations  14.2 us (1%)
    all_gather x10, waiting for transfers between devices, gather(): return lax.all_gather(arr, axes, axis=axis, tiled=True)  388 us
    dot_general x4, matrix products, layers_fn(): jnp.einsum('td,gdf->gtf', h, w_ins[c], preferred_element_type=jnp.float32)  180 us
    dot_general x24, matrix products, layers_fn(): jnp.einsum('tr,yrc->ytc', joined[g], w_outs[c][g], preferred_element_type...  172 us
    dot_general x4, matrix products, attention(): jnp.einsum('bgqk,bkc->gbqc', probs, v_all, preferred_element_type=jnp.flo...  76.9 us
    sub x4, matrix products, attention(): probs = jax.nn.softmax(scores, axis=-1).astype(jnp.bfloat16)  62.4 us
    slice x3, local copies, waits for them, and re-layouts, layers_fn(): w_outs[c][g]  56.9 us
    reshape x4, local copies, waits for them, and re-layouts, layers_fn(): z = jnp.concatenate(zs, axis=-1).transpose(1, 0, 2).reshape(rows, d_model)  41.4 us
    convert_element_type x3, other arithmetic, layers_fn(): m = (jax.nn.silu(gate) * up).astype(jnp.bfloat16)  37.8 us
  transfers between devices with their start and end apart: 10, of which 7 were waited for; matrix products, arithmetic and copies ran while one was open for 46% of the time, Pallas kernels for 0%

profile of v1, /device:TPU:97, one launch (start us, length us, event | category | flops | bytes accessed | tf_op | source)
XLA Modules:
  0.0 1159.0 jit_solution(11569217777249689946)
XLA Ops:
  22.8 27.6 %all-gather.18.cloned.1.call-done = bf16[2,2048,384]{2,1,0:T(8,128)(2,1)} async-done(((bf16[2,512,384]{2,1,0:T(8,128)(2,1)}), bf16[2,2048,384]{2,1,0:T(8,128)(2,1)}) %all-gather.18.cloned.1.call-update) | async-done | bytes 3145744 | tf_op jit(solution)/shard_map/all_gather | solution.py:39
  64.3 10.7 reshape.424
  86.7 43.8 %all-gather.34.cloned.1.call-done = bf16[1,40960,256]{2,1,0:T(8,128)(2,1)} async-done(((bf16[1,1280,256]{2,1,0:T(8,128)(2,1)}), bf16[1,40960,256]{2,1,0:T(8,128)(2,1)}) %all-gather.34.cloned.1.call-update) | async-done | bytes 20971536 | tf_op jit(solution)/shard_map/all_gather | solution.py:39
  130.4 14.9 %fusion.181 = (bf16[1,5120,256]{2,1,0:T(8,128)(2,1)}, bf16[1,5120,256]{2,1,0:T(8,128)(2,1)}, bf16[1,5120,256]{2,1,0:T(8,128)(2,1)}, bf16[1,5120,256]{2,1,0:T(8,1...) fusion(bf16[1,40960,256]{2,1,0:T(8,128)(2,1)} %all-gather.34.cl, ...), kind=kLoop, calls=%fused_computation.194 | loop fusion | bytes 41943040 | tf_op jit(solution)/shard_map/slice | solution.py:89
  145.3 63.9 %all-gather.36.cloned.1.call-done = bf16[1,40960,256]{2,1,0:T(8,128)(2,1)} async-done(((bf16[1,1280,256]{2,1,0:T(8,128)(2,1)}), bf16[1,40960,256]{2,1,0:T(8,128)(2,1)}) %all-gather.36.cloned.1.call-update) | async-done | bytes 20971536 | tf_op jit(solution)/shard_map/all_gather | solution.py:39
  209.2 14.9 %fusion.182 = (bf16[1,5120,256]{2,1,0:T(8,128)(2,1)}, bf16[1,5120,256]{2,1,0:T(8,128)(2,1)}, bf16[1,5120,256]{2,1,0:T(8,128)(2,1)}, bf16[1,5120,256]{2,1,0:T(8,1...) fusion(bf16[1,40960,256]{2,1,0:T(8,128)(2,1)} %all-gather.36.cl, ...), kind=kLoop, calls=%fused_computation.195 | loop fusion | bytes 41943040 | tf_op jit(solution)/shard_map/slice | solution.py:89
  224.1 106.0 %all-gather.24.cloned.1.call-done = bf16[1,16384,1152]{2,1,0:T(8,128)(2,1)} async-done(((bf16[1,512,1152]{2,1,0:T(8,128)(2,1)}), bf16[1,16384,1152]{2,1,0:T(8,128)(2,1)}) %all-gather.24.cloned.1.call-update) | async-done | bytes 37748752 | tf_op jit(solution)/shard_map/all_gather | solution.py:39
  330.1 44.0 %fusion.44 = bf16[8,1024,1152]{2,1,0:T(8,128)(2,1)S(1)} fusion(bf16[1024,2048,1]{1,0,2:T(8,128)(2,1)} %bitcast.272, bf16[8,2048,1152]{2,1,0:T(8,128)(2,1)} %bitcast.305), kind=kOutput, calls=%fused_computation.70 | convolution fusion | flops 38664142848 | bytes 60817408 | tf_op jit(solution)/shard_map/td,gdf->gtf/dot_general | solution.py:77
  381.0 12.6 %fusion.190 = f32[8,8,128]{2,1,0:T(8,128)S(1)} fusion(pred[8,128,1024]{2,1,0:T(8,128)(4,1)S(1)} %broadcast_and_fusion, bf16[8,8,128,128]{3,2,1,0:T(8,128)(2,1)S(1)} %bitcast.297, bf16[8,1024,256]{2,1,0:T(8,128)(2,1)} %all-gather.20.cloned.1.call-done), kind=kOutput, calls=%fused_computation.199 | convolution fusion | flops 2181039104 | bytes 5275648 | tf_op jit(solution)/shard_map/sub | solution.py:27
  393.6 19.4 %convert_bitcast_fusion.3 = bf16[8,8,128,128]{3,2,0,1:T(8,128)(2,1)} fusion(f32[8,8,128]{2,1,0:T(8,128)S(1)} %fusion.190, pred[8,128,1024]{2,1,0:T(8,128)(4,1)S(1)} %broadcast_and_fusion, bf16[8,1024,256]{2,1,0:T(8,128)(2,1)} %all-gather.20.cloned.1.call-done, bf16[8,8,128,128]{3,2,1,0:T(8,128)(2,1)S(1)} %bitcast.298), kind=kOutput, calls=%fused_computation.141 | convolution fusion | flops 4337968128 | bytes 9469952 | tf_op jit(solution)/shard_map/bgqk,bkc->gbqc/dot_general | solution.py:28
  416.4 65.3 %all-gather.26.cloned.1.call-done = bf16[1,16384,1152]{2,1,0:T(8,128)(2,1)} async-done(((bf16[1,512,1152]{2,1,0:T(8,128)(2,1)}), bf16[1,16384,1152]{2,1,0:T(8,128)(2,1)}) %all-gather.26.cloned.1.call-update) | async-done | bytes 37748752 | tf_op jit(solution)/shard_map/all_gather | solution.py:39
  481.7 44.0 %fusion.45 = bf16[8,1024,1152]{2,1,0:T(8,128)(2,1)S(1)} fusion(bf16[1024,2048,1]{1,0,2:T(8,128)(2,1)} %bitcast.273, bf16[8,2048,1152]{2,1,0:T(8,128)(2,1)} %bitcast.306), kind=kOutput, calls=%fused_computation.71 | convolution fusion | flops 38664142848 | bytes 60817408 | tf_op jit(solution)/shard_map/td,gdf->gtf/dot_general | solution.py:77
  533.7 24.3 %fusion.185 = f32[8,8,128]{2,1,0:T(8,128)S(1)} fusion(pred[8,128,1024]{2,1,0:T(8,128)(4,1)S(1)} %broadcast_and_fusion, bf16[8,8,128,128]{3,2,1,0:T(8,128)(2,1)S(1)} %bitcast.299, bf16[8,1024,256]{2,1,0:T(8,128)(2,1)} %all-gather.20.cloned.1.call-done), kind=kOutput, calls=%fused_computation.198 | convolution fusion | flops 2181039104 | bytes 5275648 | tf_op jit(solution)/shard_map/sub | solution.py:27
  558.1 18.4 %convert_bitcast_fusion.2 = bf16[8,8,128,128]{3,2,0,1:T(8,128)(2,1)S(1)} fusion(f32[8,8,128]{2,1,0:T(8,128)S(1)} %fusion.185, pred[8,128,1024]{2,1,0:T(8,128)(4,1)S(1)} %broadcast_and_fusion, bf16[8,1024,256]{2,1,0:T(8,128)(2,1)} %all-gather.20.cloned.1.call-done, bf16[8,8,128,128]{3,2,1,0:T(8,128)(2,1)} %bitcast.300), kind=kOutput, calls=%fused_computation.140 | convolution fusion | flops 4337968128 | bytes 9469952 | tf_op jit(solution)/shard_map/bgqk,bkc->gbqc/dot_general | solution.py:28
  576.7 15.4 %fusion.34 = (bf16[8,1024,512]{2,1,0:T(8,128)(2,1)S(1)}, bf16[8,1024,512]{2,1,0:T(8,128)(2,1)S(1)}) fusion(bf16[8,1024,1152]{2,1,0:T(8,128)(2,1)} %copy-done.3, bf16[8,1024,1152]{2,1,0:T(8,128)(2,1)} %copy-done.2), kind=kLoop, calls=%fused_computation.60 | loop fusion | flops 67108864 | bytes 50331648 | tf_op jit(solution)/shard_map/convert_element_type | solution.py:80
  600.7 12.7 %all-gather.28.cloned.1.call-done = bf16[1,40960,512]{2,1,0:T(8,128)(2,1)} async-done(((bf16[1,1280,512]{2,1,0:T(8,128)(2,1)}), bf16[1,40960,512]{2,1,0:T(8,128)(2,1)}) %all-gather.28.cloned.1.call-update) | async-done | bytes 41943056 | tf_op jit(solution)/shard_map/all_gather | solution.py:39
  613.4 27.1 %fusion.180 = (bf16[1,5120,512]{2,1,0:T(8,128)(2,1)S(1)}, bf16[1,5120,512]{2,1,0:T(8,128)(2,1)}, bf16[1,5120,512]{2,1,0:T(8,128)(2,1)}, bf16[1,5120,512]{2,1,0:T...) fusion(bf16[1,40960,512]{2,1,0:T(8,128)(2,1)} %all-gather.28.cl, ...), kind=kLoop, calls=%fused_computation.193 | loop fusion | bytes 83886080 | tf_op jit(solution)/shard_map/slice | solution.py:89
  640.6 10.7 fusion.83
  651.3 11.3 fusion.82
  712.2 19.5 %convert_reduce_fusion = (f32[1024]{0:T(1024)S(1)}, bf16[1024,4,512]{0,2,1:T(8,128)(2,1)S(1)}, f32[1024,4,512]{0,2,1:T(8,128)}) fusion(f32[1024,4,512]{0,2,1:T(8,128)} %copy.87, bf16[4,1280,512]{2,1,0:T(8,128)(2,1)S(1)} %bitcast.263, bf16[8,1024,1280]{2,1,0:T(8,128)(2,1)} %pad_maximum_fusion, bf16[1024,4,512]{0,2,1:T(8,128)(2,1)} %fusion.77, ...), kind=kOutput, calls=%fused_computation.75 | convolution fusion | flops 5410651136 | bytes 58200064 | tf_op jit(solution)/shard_map/tr,yrc->ytc/dot_general | solution.py:89
  739.6 47.2 %fusion.46 = bf16[8,1024,1152]{2,1,0:T(8,128)(2,1)} fusion(bf16[1024,2048,1]{0,1,2:T(8,128)(2,1)} %bitcast.275, bf16[8,2048,1152]{2,1,0:T(8,128)(2,1)} %bitcast.304), kind=kOutput, calls=%fused_computation.72 | convolution fusion | flops 38664142848 | bytes 60817408 | tf_op jit(solution)/shard_map/td,gdf->gtf/dot_general | solution.py:77
  786.8 68.2 %all-gather.32.cloned.1.call-done = bf16[1,16384,1152]{2,1,0:T(8,128)(2,1)} async-done(((bf16[1,512,1152]{2,1,0:T(8,128)(2,1)}), bf16[1,16384,1152]{2,1,0:T(8,128)(2,1)}) %all-gather.32.cloned.1.call-update) | async-done | bytes 37748752 | tf_op jit(solution)/shard_map/all_gather | solution.py:39
  855.1 45.2 %fusion.47 = bf16[8,1024,1152]{2,1,0:T(8,128)(2,1)S(1)} fusion(bf16[1024,2048,1]{0,1,2:T(8,128)(2,1)} %bitcast.276, bf16[8,2048,1152]{2,1,0:T(8,128)(2,1)} %bitcast.303), kind=kOutput, calls=%fused_computation.73 | convolution fusion | flops 38664142848 | bytes 60817408 | tf_op jit(solution)/shard_map/td,gdf->gtf/dot_general | solution.py:77
  928.9 11.2 fusion.33
  940.1 11.2 fusion.32
  951.4 12.9 %fusion.200 = f32[8,8,128]{2,1,0:T(8,128)S(1)} fusion(pred[8,128,1024]{2,1,0:T(8,128)(4,1)S(1)} %copy-done.26, bf16[8,8,128,128]{3,2,1,0:T(8,128)(2,1)} %bitcast.295, bf16[8,1024,256]{2,1,0:T(8,128)(2,1)} %all-gather.22.cloned.1.call-done), kind=kOutput, calls=%fused_computation.201 | convolution fusion | flops 2181039104 | bytes 5275648 | tf_op jit(solution)/shard_map/sub | solution.py:27
  964.2 19.6 %convert_bitcast_fusion.1 = bf16[8,8,128,128]{3,2,0,1:T(8,128)(2,1)} fusion(f32[8,8,128]{2,1,0:T(8,128)S(1)} %fusion.200, pred[8,128,1024]{2,1,0:T(8,128)(4,1)S(1)} %copy-done.26, bf16[8,1024,256]{2,1,0:T(8,128)(2,1)} %all-gather.22.cloned.1.call-done, bf16[8,8,128,128]{3,2,1,0:T(8,128)(2,1)} %bitcast.296), kind=kOutput, calls=%fused_computation.139 | convolution fusion | flops 4337968128 | bytes 9469952 | tf_op jit(solution)/shard_map/bgqk,bkc->gbqc/dot_general | solution.py:28
  987.0 12.6 %fusion.195 = f32[8,8,128]{2,1,0:T(8,128)S(1)} fusion(pred[8,128,1024]{2,1,0:T(8,128)(4,1)S(1)} %copy-done.26, bf16[8,8,128,128]{3,2,1,0:T(8,128)(2,1)S(1)} %bitcast.293, bf16[8,1024,256]{2,1,0:T(8,128)(2,1)} %all-gather.22.cloned.1.call-done), kind=kOutput, calls=%fused_computation.200 | convolution fusion | flops 2181039104 | bytes 5275648 | tf_op jit(solution)/shard_map/sub | solution.py:27
  999.6 19.5 %convert_bitcast_fusion = bf16[8,8,128,128]{3,2,0,1:T(8,128)(2,1)} fusion(f32[8,8,128]{2,1,0:T(8,128)S(1)} %fusion.195, pred[8,128,1024]{2,1,0:T(8,128)(4,1)S(1)} %copy-done.26, bf16[8,1024,256]{2,1,0:T(8,128)(2,1)} %all-gather.22.cloned.1.call-done, bf16[8,8,128,128]{3,2,1,0:T(8,128)(2,1)S(1)} %bitcast.294), kind=kOutput, calls=%fused_computation.138 | convolution fusion | flops 4337968128 | bytes 9469952 | tf_op jit(solution)/shard_map/bgqk,bkc->gbqc/dot_general | solution.py:28
  1089.3 11.0 add_bitcast_fusion.1
  1100.3 11.0 add_bitcast_fusion
  1140.4 11.5 add_convert_fusion
  (139 shorter events, 257.2 us)
Async XLA Ops:
  6.5 43.9 %all-gather.18.cloned.1.call-start = ((), (), s32[]{:S(2)}) async-start(), calls=%async_computation | async-start | bytes 3932160 | tf_op jit(solution)/shard_map/all_gather | solution.py:39
  9.5 120.9 %all-gather.34.cloned.1.call-start = ((), (), s32[]{:S(2)}) async-start(), calls=%async_computation.8 | async-start | bytes 21626880 | tf_op jit(solution)/shard_map/all_gather | solution.py:39
  12.1 197.1 %all-gather.36.cloned.1.call-start = ((), (), s32[]{:S(2)}) async-start(), calls=%async_computation.9 | async-start | bytes 21626880 | tf_op jit(solution)/shard_map/all_gather | solution.py:39
  12.9 317.1 %all-gather.24.cloned.1.call-start = ((), (), s32[]{:S(2)}) async-start(), calls=%async_computation.3 | async-start | bytes 38928384 | tf_op jit(solution)/shard_map/all_gather | solution.py:39
  17.7 363.4 %all-gather.20.cloned.1.call-start = ((), (), s32[]{:S(2)}) async-start(), calls=%async_computation.1 | async-start | bytes 4718592 | tf_op jit(solution)/shard_map/all_gather | solution.py:39
  57.0 4.2 copy-start.23
  60.5 421.2 %all-gather.26.cloned.1.call-start = ((), (), s32[]{:S(2)}) async-start(), calls=%async_computation.4 | async-start | bytes 38928384 | tf_op jit(solution)/shard_map/all_gather | solution.py:39
  61.1 552.3 %all-gather.28.cloned.1.call-start = ((), (), s32[]{:S(2)}) async-start(), calls=%async_computation.5 | async-start | bytes 43253760 | tf_op jit(solution)/shard_map/all_gather | solution.py:39
  62.4 677.2 %all-gather.30.cloned.1.call-start = ((), (), s32[]{:S(2)}) async-start(), calls=%async_computation.6 | async-start | bytes 38928384 | tf_op jit(solution)/shard_map/all_gather | solution.py:39
  63.2 791.9 %all-gather.32.cloned.1.call-start = ((), (), s32[]{:S(2)}) async-start(), calls=%async_computation.7 | async-start | bytes 38928384 | tf_op jit(solution)/shard_map/all_gather | solution.py:39
  64.0 887.3 %all-gather.22.cloned.1.call-start = ((), (), s32[]{:S(2)}) async-start(), calls=%async_computation.2 | async-start | bytes 4718592 | tf_op jit(solution)/shard_map/all_gather | solution.py:39
  64.3 10.7 copy-start.28
  86.0 472.1 %copy-start.25 = (pred[8,128,1024]{2,1,0:T(8,128)(4,1)}, pred[8,128,1024]{2,1,0:T(8,128)(4,1)S(1)}, u32[]{:S(2)}) copy-start(pred[8,128,1024]{2,1,0:T(8,128)(4,1)S(1)} %broadcast_and_fusion) | copy-start | bytes 3145732
  374.1 6.6 copy-start.2
  525.7 6.4 copy-start.3
  576.6 15.5 %copy-start.5 = (bf16[8,8,128,128]{3,2,1,0:T(8,128)(2,1)S(1)}, bf16[8,8,128,128]{3,2,1,0:T(8,128)(2,1)}, u32[]{:S(2)}) copy-start(bf16[8,8,128,128]{3,2,1,0:T(8,128)(2,1)} %copy.21) | copy-start | bytes 6291460
  640.6 10.7 copy-start.1
  900.3 7.6 copy-start.4
  940.1 11.2 copy-start.26
  1021.3 9.3 copy-start.21
  1030.7 4.2 copy-start.19
  1034.9 4.2 copy-start.17
  1039.0 4.3 copy-start.15
  1043.3 4.2 copy-start.13
  1047.5 4.2 copy-start.11
  1055.8 4.2 copy-start.22
  1059.9 4.2 copy-start.20
  1064.1 4.2 copy-start.18
  1068.3 4.2 copy-start.16
  1072.5 4.4 copy-start.14
  1076.8 4.2 copy-start.12
  1081.0 4.2 copy-start.10
  (7 other events, 16.7 us)
Sparse Core Ops, SparseCore 0:
  9.6 40.7 all-gather.17
  52.5 77.8 all-gather.33
  132.5 76.5 all-gather.35
  211.2 118.8 all-gather.23
  331.5 28.7 all-gather.19
  362.3 119.3 all-gather.25
  483.8 129.5 all-gather.27
  615.6 118.6 all-gather.29
  736.4 118.6 all-gather.31
  856.5 28.7 all-gather.21

commit v2 on v1

v2 whole, which is shorter than its diff:
```python
import functools
import math
import jax
import jax.numpy as jnp
from jax import lax
from jax.experimental import pallas as pl
from jax.experimental.pallas import tpu as pltpu
from jax.sharding import PartitionSpec as P

NORM_EPS = 1e-6
NEG_BIG = -1e30
VMEM_LIMIT = 60 * 1024 * 1024
FF_TILE = 256


def layer_norm(x_act, gain_vec):
    x_f32 = x_act.astype(jnp.float32)
    centered = x_f32 - jnp.mean(x_f32, axis=-1, keepdims=True)
    variance = jnp.mean(centered * centered, axis=-1, keepdims=True)
    return (centered * lax.rsqrt(variance + NORM_EPS) * gain_vec.astype(jnp.float32)).astype(jnp.bfloat16)


def heads_kernel(n_heads, head_dim, ff_head, meta_ref, h_ref, kv_ref, w_ref, o_ref, q_ref):
    unit_in = head_dim + 2 * ff_head
    unit_out = head_dim + ff_head
    n_blocks, n_batch, t_loc, _ = kv_ref.shape
    k_len = n_blocks * t_loc
    tiles = ff_head // FF_TILE

    w_q = jnp.concatenate([w_ref[0, :, i * unit_in:i * unit_in + head_dim] for i in range(n_heads)], axis=1)
    q_ref[...] = jnp.dot(h_ref[...], w_q, preferred_element_type=jnp.float32).astype(jnp.bfloat16)

    @pl.loop(0, n_heads * tiles)
    def _(step):
        head = step // tiles
        tile = step % tiles
        g_at = pl.multiple_of(head * unit_in + head_dim + tile * FF_TILE, 128)
        u_at = pl.multiple_of(head * unit_in + head_dim + ff_head + tile * FF_TILE, 128)
        m_at = pl.multiple_of(head * unit_out + head_dim + tile * FF_TILE, 128)
        gate = jnp.dot(h_ref[...], w_ref[0, :, pl.ds(g_at, FF_TILE)], preferred_element_type=jnp.float32)
        up = jnp.dot(h_ref[...], w_ref[0, :, pl.ds(u_at, FF_TILE)], preferred_element_type=jnp.float32)
        gate = gate.astype(jnp.bfloat16).astype(jnp.float32)
        up = up.astype(jnp.bfloat16).astype(jnp.float32)
        o_ref[0, :, pl.ds(m_at, FF_TILE)] = (gate * jax.nn.sigmoid(gate) * up).astype(jnp.bfloat16)

    @pl.loop(0, n_batch)
    def _(b):
        at = pl.multiple_of(b * t_loc, t_loc)
        q = jnp.concatenate([q_ref[pl.ds(at, t_loc), i * head_dim:(i + 1) * head_dim] for i in range(n_heads)], axis=0)
        k = kv_ref[:, b, :, :head_dim].reshape(k_len, head_dim)
        v = kv_ref[:, b, :, head_dim:].reshape(k_len, head_dim)
        s = lax.dot_general(q, k, (((1,), (1,)), ((), ())), preferred_element_type=jnp.float32) * (1.0 / math.sqrt(head_dim))
        q_pos = meta_ref[n_batch] + lax.broadcasted_iota(jnp.int32, (t_loc, k_len), 0)
        k_pos = lax.broadcasted_iota(jnp.int32, (t_loc, k_len), 1)
        allowed = k_pos <= jnp.minimum(q_pos, meta_ref[b] - 1)
        s = jnp.where(jnp.concatenate([allowed] * n_heads, axis=0), s, NEG_BIG)
        e = jnp.exp(s - jnp.max(s, axis=-1, keepdims=True))
        p = (e * (1.0 / jnp.sum(e, axis=-1, keepdims=True))).astype(jnp.bfloat16)
        o = jnp.dot(p, v, preferred_element_type=jnp.float32).astype(jnp.bfloat16)
        for i in range(n_heads):
            o_ref[0, pl.ds(at, t_loc), i * unit_out:i * unit_out + head_dim] = o[i * t_loc:(i + 1) * t_loc]


def out_kernel(x_ref, a_ref, w_ref, y_ref, acc_ref):
    group = pl.program_id(1)
    col = w_ref.shape[3]

    @pl.when(group == 0)
    def _():
        acc_ref[...] = jnp.zeros_like(acc_ref)

    for c in range(w_ref.shape[1]):
        z = jnp.dot(a_ref[0], w_ref[0, c], preferred_element_type=jnp.float32)
        acc_ref[:, c * col:(c + 1) * col] += z.astype(jnp.bfloat16).astype(jnp.float32)

    @pl.when(group == pl.num_programs(1) - 1)
    def _():
        y_ref[...] = (x_ref[...].astype(jnp.float32) + acc_ref[...]).astype(jnp.bfloat16)


def project_heads(meta, h, kv, w_in, n_heads, head_dim, ff_head):
    n_groups, d_model, in_loc = w_in.shape
    rows = h.shape[0]
    out_loc = n_heads * (head_dim + ff_head)
    whole = pl.Buffered(1)
    return pl.pallas_call(
        functools.partial(heads_kernel, n_heads, head_dim, ff_head),
        grid=(n_groups,),
        in_specs=[
            pl.BlockSpec(memory_space=pltpu.SMEM),
            pl.BlockSpec(h.shape, lambda g: (0, 0), pipeline_mode=whole),
            pl.BlockSpec(kv.shape, lambda g: (0, 0, 0, 0), pipeline_mode=whole),
            pl.BlockSpec((1, d_model, in_loc), lambda g: (g, 0, 0)),
        ],
        out_specs=pl.BlockSpec((1, rows, out_loc), lambda g: (g, 0, 0)),
        out_shape=jax.ShapeDtypeStruct((n_groups, rows, out_loc), jnp.bfloat16),
        scratch_shapes=[pltpu.VMEM((rows, n_heads * head_dim), jnp.bfloat16)],
        compiler_params=pltpu.CompilerParams(vmem_limit_bytes=VMEM_LIMIT, dimension_semantics=("arbitrary",)),
        cost_estimate=pl.CostEstimate(flops=2 * rows * d_model * in_loc * n_groups, bytes_accessed=2 * w_in.size, transcendentals=0),
        name="project_heads",
    )(meta, h, kv, w_in)


def project_out(x, joined, w_out):
    n_groups, n_data, out_loc, col = w_out.shape
    rows, d_model = x.shape
    per = 2 if n_data % 2 == 0 else 1
    return pl.pallas_call(
        out_kernel,
        grid=(n_data // per, n_groups),
        in_specs=[
            pl.BlockSpec((rows, per * col), lambda c, g: (0, c)),
            pl.BlockSpec((1, rows, out_loc), lambda c, g: (g, 0, 0)),
            pl.BlockSpec((1, per, out_loc, col), lambda c, g: (g, c, 0, 0)),
        ],
        out_specs=pl.BlockSpec((rows, per * col), lambda c, g: (0, c)),
        out_shape=jax.ShapeDtypeStruct((rows, d_model), jnp.bfloat16),
        scratch_shapes=[pltpu.VMEM((rows, per * col), jnp.float32)],
        compiler_params=pltpu.CompilerParams(vmem_limit_bytes=VMEM_LIMIT, dimension_semantics=("arbitrary", "arbitrary")),
        cost_estimate=pl.CostEstimate(flops=2 * rows * d_model * out_loc * n_groups, bytes_accessed=2 * w_out.size, transcendentals=0),
        name="project_out",
    )(x, joined, w_out)


def stack_by_shift(arr, axis, size, stride):
    n = size // stride
    parts = [arr]
    for r in range(1, n):
        parts.append(lax.ppermute(arr, axis, [(i, (i + r * stride) % size) for i in range(size)]))
    return jnp.stack(parts)


def absolute_order(rel, mine, n):
    return jnp.concatenate([lax.dynamic_slice_in_dim(rel, lax.rem(mine - i + n, n), 1, 0) for i in range(n)])


def gather_model(arr, n_model):
    me = lax.axis_index("model")
    half = n_model // 2
    mine = stack_by_shift(arr, "model", n_model, 2)
    other = lax.ppermute(mine, "model", [(i, i ^ 1) for i in range(n_model)])
    first = lax.rem(me, 2) == 0
    both = jnp.stack([jnp.where(first, mine, other), jnp.where(first, other, mine)], axis=1)
    both = absolute_order(both, me // 2, half)
    return both.reshape((n_model,) + arr.shape)


def solution(mesh):
    n_model = mesh.shape["model"]
    n_data = mesh.shape["data"]
    act_spec = P(None, ("part", "data"), "model", None)
    ring = ("model", "data")

    def gather(arr):
        return lax.all_gather(arr, ring, axis=0, tiled=True)

    def layers_fn(x_blk, len_blk, gain_blk, w_in_blk, w_kv_blk, w_out_blk):
        n_layers, feat, in_loc = w_in_blk.shape
        head_dim = w_kv_blk.shape[2] // 2
        out_loc = w_out_blk.shape[1]
        heads_loc = (out_loc - (in_loc - out_loc)) // head_dim
        ff_head = out_loc // heads_loc - head_dim
        n_micro, n_seqs, t_loc, d_model = x_blk.shape
        n_batch = n_micro * n_seqs
        rows = n_batch * t_loc
        me_data = lax.axis_index("data")
        q_offset = lax.axis_index("model") * t_loc
        meta = jnp.concatenate([len_blk.reshape(n_batch), q_offset[None]]).astype(jnp.int32)

        weights = []
        for layer in range(n_layers):
            w_in = gather(w_in_blk[layer]).reshape(n_model, d_model, in_loc)
            w_out = gather(w_out_blk[layer]).reshape(n_model, n_data, out_loc, feat)
            weights.append((w_in, w_out))

        small = jnp.concatenate([w_kv_blk, jnp.broadcast_to(gain_blk[..., None], gain_blk.shape + (head_dim,))], axis=2)
        small = absolute_order(stack_by_shift(small, "data", n_data, 1), me_data, n_data)
        small = small.transpose(1, 0, 2, 3).reshape(n_layers, d_model, 3 * head_dim)

        hidden = x_blk.reshape(rows, d_model)
        for layer, (w_in, w_out) in enumerate(weights):
            h = layer_norm(hidden, small[layer, :, 2 * head_dim])
            kv = jnp.dot(h, small[layer, :, :2 * head_dim], preferred_element_type=jnp.float32).astype(jnp.bfloat16)
            kv = gather_model(kv.reshape(n_batch, t_loc, 2 * head_dim), n_model)
            joined = project_heads(meta, h, kv, w_in, heads_loc, head_dim, ff_head)
            hidden = project_out(hidden, joined, w_out)
        return hidden.reshape(x_blk.shape)

    return jax.shard_map(
        layers_fn,
        mesh=mesh,
        in_specs=(act_spec, P(None, ("part", "data")), P(None, "data"), P(None, "data", "model"), P(None, "data", None), P(None, "model", "data")),
        out_specs=act_spec,
        check_vma=False,
    )
```

time: 1170 us -> 848 us (0.72)
  matrix products: 498 us -> 2.52 us
  Pallas kernels: 0 us -> 396 us
  local copies, waits for them, and re-layouts: 166 us -> 11.2 us
  other arithmetic: 89.7 us -> 28.7 us
  starting transfers between devices: 0.74 us -> 26.1 us
  waiting for transfers between devices: 391 us -> 370 us
    dot_general x32 -> x0, matrix products: 429 us -> none  [the longest x4 180 us: layers_fn(): jnp.einsum('td,gdf->gtf', h, w_ins[c], preferred_element_type=jnp.float32)]
    pallas_call x0 -> x4, Pallas kernels: none -> 396 us  [the longest x2 290 us: project_heads(): pl.pallas_call(functools.partial(heads_kernel, n_heads, head_dim, ff_head...]
    all_gather x10 -> x4, waiting for transfers between devices: 388 us -> 232 us  [gather(): return lax.all_gather(arr, ring, axis=0, tiled=True)]
    ppermute x0 -> x11, waiting for transfers between devices: none -> 137 us  [the longest x9 131 us: stack_by_shift(): lax.ppermute(arr, axis, [(i, (i + r * stride) % size) for i in range(size)])]
    slice x10 -> x2, local copies, waits for them, and re-layouts: 71.5 us -> 6.68 us  [the longest x1 4.95 us: layers_fn(): w_in = gather(w_in_blk[layer]).reshape(n_model, d_model, in_loc)]
    sub x4 -> x0, matrix products: 62.4 us -> none  [attention(): probs = jax.nn.softmax(scores, axis=-1).astype(jnp.bfloat16)]
    convert_element_type x4 -> x0, other arithmetic: 49.4 us -> none  [the longest x3 37.8 us: layers_fn(): m = (jax.nn.silu(gate) * up).astype(jnp.bfloat16)]
    reshape x4 -> x1, local copies, waits for them, and re-layouts: 41.4 us -> 0.08 us  [layers_fn(): len_blk.reshape(n_batch)]
  transfers between devices with their start and end apart: 10 -> 15, of which waited for: 7 -> 11; matrix products, arithmetic and copies ran while one was open for 46% -> 4% of each run, Pallas kernels for 0% -> 41%
where the time goes in v2:
time: 848 us
  Pallas kernels  396 us (47%)
  waiting for transfers between devices  370 us (44%)
  other arithmetic  28.7 us (3%)
  starting transfers between devices  26.1 us (3%)
  between operations  13.4 us (2%)
  local copies, waits for them, and re-layouts  11.2 us (1%)
    pallas_call x2, Pallas kernels, project_heads(): pl.pallas_call(functools.partial(heads_kernel, n_heads, head_dim, ff_head...  290 us
    all_gather x4, waiting for transfers between devices, gather(): return lax.all_gather(arr, ring, axis=0, tiled=True)  232 us
    ppermute x9, waiting for transfers between devices, stack_by_shift(): lax.ppermute(arr, axis, [(i, (i + r * stride) % size) for i in range(size)])  131 us
    pallas_call x2, Pallas kernels, project_out(): pl.pallas_call(out_kernel, grid=(n_data // per, n_groups), in_specs=[pl.B...  106 us
  transfers between devices with their start and end apart: 15, of which 11 were waited for; matrix products, arithmetic and copies ran while one was open for 4% of the time, Pallas kernels for 41%

profile of v2, /device:TPU:97, one launch (start us, length us, event | category | flops | bytes accessed | tf_op | source)
XLA Modules:
  0.0 848.2 jit_solution(3836665459019104990)
XLA Ops:
  6.6 5.0 fusion.19
  11.7 1.7 fusion.20
  15.1 1.3 fusion.18
  16.4 5.2 collective-permute-start.2
  22.8 3.8 convert_reduce_fusion.1
  28.7 24.0 %collective-permute-done.2 = bf16[2,512,384]{2,1,0:T(8,128)(2,1)S(1)} collective-permute-done((bf16[2,512,384]{2,1,0:T(8,128)(2,1)}, bf16[2,512,384]{2,1,0:T(8,128)(2,1)S(1)}, u32[]{:S(2)}, u32[]{:S(2)}) %collective-permute-start.2) | collective-permute-done | bytes 786464 | tf_op jit(solution)/shard_map/ppermute | solution.py:129
  53.8 30.0 %collective-permute-done.1 = bf16[2,512,384]{2,1,0:T(8,128)(2,1)S(1)} collective-permute-done((bf16[2,512,384]{2,1,0:T(8,128)(2,1)}, bf16[2,512,384]{2,1,0:T(8,128)(2,1)S(1)}, u32[]{:S(2)}, u32[]{:S(2)}) %collective-permute-start.1) | collective-permute-done | bytes 786464 | tf_op jit(solution)/shard_map/ppermute | solution.py:129
  85.5 1.4 fusion.9
  88.3 1.3 collective-permute-start.3
  89.6 3.0 collective-permute-start.4
  93.5 6.3 collective-permute-done.3
  99.8 18.3 %collective-permute-done.4 = bf16[8,128,256]{2,1,0:T(8,128)(2,1)S(1)} collective-permute-done((bf16[8,128,256]{2,1,0:T(8,128)(2,1)S(1)}, bf16[8,128,256]{2,1,0:T(8,128)(2,1)S(1)}, u32[]{:S(2)}, u32[]{:S(2)}) %collective-permute-start.4) | collective-permute-done | bytes 524320 | tf_op jit(solution)/shard_map/ppermute | solution.py:129
  118.1 6.4 collective-permute-done.5
  124.5 1.6 pad_maximum_fusion.4
  126.1 8.0 collective-permute-start.6
  134.8 4.5 multiply_convert_fusion.h_ref
  139.4 1.8 select_bitcast_fusion.2
  142.1 2.3 copy.12
  144.4 125.7 %all-gather.9.cloned.1.call-done = bf16[1,16384,2304]{2,1,0:T(8,128)(2,1)} async-done(((bf16[1,512,2304]{2,1,0:T(8,128)(2,1)}), bf16[1,16384,2304]{2,1,0:T(8,128)(2,1)}) %all-gather.9.cloned.1.call-update) | async-done | bytes 75497488 | tf_op jit(solution)/shard_map/all_gather | solution.py:155
  270.1 145.1 %project_heads.2.a_ref = bf16[8,1024,1280]{2,1,0:T(8,128)(2,1)} custom-call(s32[9]{0:T(128)} %pad_add_fusion.meta_ref, bf16[1024,2048]{1,0:T(8,128)(2,1)} %multiply_convert_fusion.h_ref, bf16[8,8,128,256]{3,2,1,0:T(8,128)(2,1)} %bitcast.60, bf16[8,2048,2304]{2,1,0:T(8,128)(2,1)} %bitcast.24.w_ref), custom_call_target="tpu_custom_call" | custom-call | flops 77309411328 | bytes 75497472 | tf_op jit(solution)/shard_map/project_heads/pallas_call | solution.py:86
  415.2 53.6 %project_out.2.x_ref = bf16[1024,2048]{1,0:T(8,128)(2,1)} custom-call(bf16[1024,2048]{1,0:T(8,128)(2,1)} %bitcast.55, bf16[8,1024,1280]{2,1,0:T(8,128)(2,1)} %project_heads.2.a_ref, bf16[8,4,1280,512]{3,2,1,0:T(8,128)(2,1)} %bitcast.90), custom_call_target="tpu_custom_call" | custom-call | flops 42949672960 | bytes 41943040 | tf_op jit(solution)/shard_map/project_out/pallas_call | solution.py:108
  468.9 3.8 convert_reduce_fusion
  474.4 1.6 fusion.6.h_ref
  477.4 1.5 collective-permute-start.7
  478.8 2.4 collective-permute-start.8
  482.4 21.5 %collective-permute-done.7 = bf16[8,128,256]{2,1,0:T(8,128)(2,1)S(1)} collective-permute-done((bf16[8,128,256]{2,1,0:T(8,128)(2,1)S(1)}, bf16[8,128,256]{2,1,0:T(8,128)(2,1)S(1)}, u32[]{:S(2)}, u32[]{:S(2)}) %collective-permute-start.7) | collective-permute-done | bytes 524320 | tf_op jit(solution)/shard_map/ppermute | solution.py:129
  503.9 23.4 %collective-permute-done.8 = bf16[8,128,256]{2,1,0:T(8,128)(2,1)S(1)} collective-permute-done((bf16[8,128,256]{2,1,0:T(8,128)(2,1)S(1)}, bf16[8,128,256]{2,1,0:T(8,128)(2,1)S(1)}, u32[]{:S(2)}, u32[]{:S(2)}) %collective-permute-start.8) | collective-permute-done | bytes 524320 | tf_op jit(solution)/shard_map/ppermute | solution.py:129
  528.8 6.1 collective-permute-done.10
  535.8 2.3 pad_maximum_fusion.1
  538.1 106.1 %all-gather.13.cloned.1.call-done = bf16[1,16384,2304]{2,1,0:T(8,128)(2,1)} async-done(((bf16[1,512,2304]{2,1,0:T(8,128)(2,1)}), bf16[1,16384,2304]{2,1,0:T(8,128)(2,1)}) %all-gather.13.cloned.1.call-update) | async-done | bytes 75497488 | tf_op jit(solution)/shard_map/all_gather | solution.py:155
  644.1 145.0 %project_heads.3.a_ref = bf16[8,1024,1280]{2,1,0:T(8,128)(2,1)} custom-call(s32[9]{0:T(128)} %pad_add_fusion.meta_ref, bf16[1024,2048]{1,0:T(8,128)(2,1)} %copy-done.2, bf16[8,8,128,256]{3,2,1,0:T(8,128)(2,1)} %bitcast.59, bf16[8,2048,2304]{2,1,0:T(8,128)(2,1)} %bitcast.36.w_ref), custom_call_target="tpu_custom_call" | custom-call | flops 77309411328 | bytes 75497472 | tf_op jit(solution)/shard_map/project_heads/pallas_call | solution.py:86
  789.2 52.5 %project_out.3 = bf16[1024,2048]{1,0:T(8,128)(2,1)} custom-call(bf16[1024,2048]{1,0:T(8,128)(2,1)} %project_out.2.x_ref, bf16[8,1024,1280]{2,1,0:T(8,128)(2,1)} %project_heads.3.a_ref, bf16[8,4,1280,512]{3,2,1,0:T(8,128)(2,1)} %bitcast.89), custom_call_target="tpu_custom_call" | custom-call | flops 42949672960 | bytes 41943040 | tf_op jit(solution)/shard_map/project_out/pallas_call | solution.py:108
  (70 shorter events, 18.4 us)
Async XLA Ops:
  6.5 5.1 copy-start.4
  6.5 263.6 %all-gather.9.cloned.1.call-start = ((), (), s32[]{:S(2)}) async-start(), calls=%async_computation | async-start | bytes 77856768 | tf_op jit(solution)/shard_map/all_gather | solution.py:155
  11.6 3.3 copy-start.14
  11.6 3.5 copy-start.13
  11.6 403.7 %all-gather.11.cloned.1.call-start = ((), (), s32[]{:S(2)}) async-start(), calls=%async_computation.1 | async-start | bytes 43253760 | tf_op jit(solution)/shard_map/all_gather | solution.py:155
  13.5 630.7 %all-gather.13.cloned.1.call-start = ((), (), s32[]{:S(2)}) async-start(), calls=%async_computation.2 | async-start | bytes 77856768 | tf_op jit(solution)/shard_map/all_gather | solution.py:155
  14.3 774.9 %all-gather.15.cloned.1.call-start = ((), (), s32[]{:S(2)}) async-start(), calls=%async_computation.3 | async-start | bytes 43253760 | tf_op jit(solution)/shard_map/all_gather | solution.py:155
  16.4 36.3 %collective-permute-start.2 = (bf16[2,512,384]{2,1,0:T(8,128)(2,1)}, bf16[2,512,384]{2,1,0:T(8,128)(2,1)S(1)}, u32[]{:S(2)}, u32[]{:S(2)}) collective-permute-start(bf16[2,512,384]{2,1,0:T(8,128)(2,1)} %get-tuple-element.28), channel_id=1, source_target_pairs={{0,24},{8,0},{16,8},{24,16},{1,25},{9,1},{17,9},{25,17},{2,26},{10... | collective-permute-start | bytes 2359304 | tf_op jit(solution)/shard_map/ppermute | solution.py:129
  21.6 32.2 %collective-permute-start = (bf16[2,512,384]{2,1,0:T(8,128)(2,1)}, bf16[2,512,384]{2,1,0:T(8,128)(2,1)S(1)}, u32[]{:S(2)}, u32[]{:S(2)}) collective-permute-start(bf16[2,512,384]{2,1,0:T(8,128)(2,1)} %get-tuple-element.28), channel_id=1, source_target_pairs={{0,8},{8,16},{16,24},{24,0},{1,9},{9,17},{17,25},{25,1},{2,10},{10... | collective-permute-start | bytes 2359304 | tf_op jit(solution)/shard_map/ppermute | solution.py:129
  21.6 62.2 %collective-permute-start.1 = (bf16[2,512,384]{2,1,0:T(8,128)(2,1)}, bf16[2,512,384]{2,1,0:T(8,128)(2,1)S(1)}, u32[]{:S(2)}, u32[]{:S(2)}) collective-permute-start(bf16[2,512,384]{2,1,0:T(8,128)(2,1)} %get-tuple-element.28), channel_id=1, source_target_pairs={{0,16},{8,24},{16,0},{24,8},{1,17},{9,25},{17,1},{25,9},{2,18},{10... | collective-permute-start | bytes 2359304 | tf_op jit(solution)/shard_map/ppermute | solution.py:129
  22.8 4.7 copy-start
  22.8 61.0 %copy-start.3 = (bf16[1,2,512,384]{3,2,0,1:T(8,128)(2,1)S(1)}, bf16[1,2,512,384]{3,2,0,1:T(8,128)(2,1)}, u32[]{:S(2)}) copy-start(bf16[1,2,512,384]{3,2,0,1:T(8,128)(2,1)} %get-tuple-element.27) | copy-start | bytes 2359300
  87.0 47.1 %copy-start.15 = (s32[2,4]{1,0:T(2,128)S(1)}, s32[2,4]{1,0:T(2,128)}, u32[]{:S(2)}) copy-start(s32[2,4]{1,0:T(2,128)} %param.7) | copy-start | bytes 100
  88.3 36.2 %copy-start.5 = (bf16[1024,256]{1,0:T(8,128)(2,1)}, bf16[1024,256]{1,0:T(8,128)(2,1)S(1)}, u32[]{:S(2)}) copy-start(bf16[1024,256]{1,0:T(8,128)(2,1)S(1)} %convolution_convert_fusion.1) | copy-start | bytes 1572868
  88.3 11.5 %collective-permute-start.3 = (bf16[8,128,256]{2,1,0:T(8,128)(2,1)S(1)}, bf16[8,128,256]{2,1,0:T(8,128)(2,1)S(1)}, u32[]{:S(2)}, u32[]{:S(2)}) collective-permute-start(bf16[8,128,256]{2,1,0:T(8,128)(2,1)S(1)} %bitcast.62), channel_id=1, source_target_pairs={{0,2},{1,3},{2,4},{3,5},{4,6},{5,7},{6,0},{7,1},{8,10},{9,11},{10,... | collective-permute-start | bytes 1572872 | tf_op jit(solution)/shard_map/ppermute | solution.py:129
  89.6 28.5 %collective-permute-start.4 = (bf16[8,128,256]{2,1,0:T(8,128)(2,1)S(1)}, bf16[8,128,256]{2,1,0:T(8,128)(2,1)S(1)}, u32[]{:S(2)}, u32[]{:S(2)}) collective-permute-start(bf16[8,128,256]{2,1,0:T(8,128)(2,1)S(1)} %bitcast.63), channel_id=1, source_target_pairs={{0,4},{1,5},{2,6},{3,7},{4,0},{5,1},{6,2},{7,3},{8,12},{9,13},{10,... | collective-permute-start | bytes 1572872 | tf_op jit(solution)/shard_map/ppermute | solution.py:129
  92.6 31.8 %collective-permute-start.5 = (bf16[8,128,256]{2,1,0:T(8,128)(2,1)S(1)}, bf16[8,128,256]{2,1,0:T(8,128)(2,1)S(1)}, u32[]{:S(2)}, u32[]{:S(2)}) collective-permute-start(bf16[8,128,256]{2,1,0:T(8,128)(2,1)S(1)} %bitcast.64), channel_id=1, source_target_pairs={{0,6},{1,7},{2,0},{3,1},{4,2},{5,3},{6,4},{7,5},{8,14},{9,15},{10,... | collective-permute-start | bytes 1572872 | tf_op jit(solution)/shard_map/ppermute | solution.py:129
  99.8 26.3 %copy-start.7 = (bf16[8,128,256]{2,1,0:T(8,128)(2,1)}, bf16[8,128,256]{2,1,0:T(8,128)(2,1)S(1)}, u32[]{:S(2)}) copy-start(bf16[8,128,256]{2,1,0:T(8,128)(2,1)S(1)} %collective-permute-done.3) | copy-start | bytes 1572868
  118.1 8.0 copy-start.9
  124.4 1.6 copy-start.11
  126.1 13.3 %collective-permute-start.6 = (bf16[4,8,128,256]{3,2,1,0:T(8,128)(2,1)}, bf16[4,8,128,256]{3,2,1,0:T(8,128)(2,1)}, u32[]{:S(2)}, u32[]{:S(2)}) collective-permute-start(bf16[4,8,128,256]{3,2,1,0:T(8,128)(2,1)} %pad_maximum_fusion.4), channel_id=1, source_target_pairs={{0,1},{1,0},{2,3},{3,2},{4,5},{5,4},{6,7},{7,6},{8,9},{9,8},{10,11... | collective-permute-start | bytes 6291464 | tf_op jit(solution)/shard_map/ppermute | solution.py:141
  134.8 4.6 copy-start.6
  134.8 4.6 copy-start.8
  134.8 4.6 copy-start.10
  134.8 4.6 copy-start.12
  468.9 4.4 copy-start.1
  476.1 51.5 %copy-start.2 = (bf16[1024,2048]{1,0:T(8,128)(2,1)}, bf16[1024,2048]{1,0:T(8,128)(2,1)S(1)}, u32[]{:S(2)}) copy-start(bf16[1024,2048]{1,0:T(8,128)(2,1)S(1)} %fusion.6.h_ref) | copy-start | bytes 12582916
  477.4 26.5 %collective-permute-start.7 = (bf16[8,128,256]{2,1,0:T(8,128)(2,1)S(1)}, bf16[8,128,256]{2,1,0:T(8,128)(2,1)S(1)}, u32[]{:S(2)}, u32[]{:S(2)}) collective-permute-start(bf16[8,128,256]{2,1,0:T(8,128)(2,1)S(1)} %bitcast.73), channel_id=1, source_target_pairs={{0,2},{1,3},{2,4},{3,5},{4,6},{5,7},{6,0},{7,1},{8,10},{9,11},{10,... | collective-permute-start | bytes 1572872 | tf_op jit(solution)/shard_map/ppermute | solution.py:129
  478.8 48.5 %collective-permute-start.8 = (bf16[8,128,256]{2,1,0:T(8,128)(2,1)S(1)}, bf16[8,128,256]{2,1,0:T(8,128)(2,1)S(1)}, u32[]{:S(2)}, u32[]{:S(2)}) collective-permute-start(bf16[8,128,256]{2,1,0:T(8,128)(2,1)S(1)} %bitcast.74), channel_id=1, source_target_pairs={{0,4},{1,5},{2,6},{3,7},{4,0},{5,1},{6,2},{7,3},{8,12},{9,13},{10,... | collective-permute-start | bytes 1572872 | tf_op jit(solution)/shard_map/ppermute | solution.py:129
  481.3 46.1 %collective-permute-start.9 = (bf16[8,128,256]{2,1,0:T(8,128)(2,1)S(1)}, bf16[8,128,256]{2,1,0:T(8,128)(2,1)S(1)}, u32[]{:S(2)}, u32[]{:S(2)}) collective-permute-start(bf16[8,128,256]{2,1,0:T(8,128)(2,1)S(1)} %bitcast.75), channel_id=1, source_target_pairs={{0,6},{1,7},{2,0},{3,1},{4,2},{5,3},{6,4},{7,5},{8,14},{9,15},{10,... | collective-permute-start | bytes 1572872 | tf_op jit(solution)/shard_map/ppermute | solution.py:129
  527.6 7.3 collective-permute-start.10
Sparse Core Ops, SparseCore 0:
  11.7 258.4 all-gather.8
  272.3 132.1 all-gather.10
  406.6 237.5 all-gather.12
  646.1 129.4 all-gather.14

commit v3 on v2

v3 whole, which is shorter than its diff:
```python
import functools
import math
import jax
import jax.numpy as jnp
from jax import lax
from jax.experimental import pallas as pl
from jax.experimental.pallas import tpu as pltpu
from jax.sharding import PartitionSpec as P

NORM_EPS = 1e-6
NEG_BIG = -1e30
VMEM_LIMIT = 60 * 1024 * 1024
FF_TILE = 256


def layer_norm(x_act, gain_vec):
    x_f32 = x_act.astype(jnp.float32)
    centered = x_f32 - jnp.mean(x_f32, axis=-1, keepdims=True)
    variance = jnp.mean(centered * centered, axis=-1, keepdims=True)
    return (centered * lax.rsqrt(variance + NORM_EPS) * gain_vec.astype(jnp.float32)).astype(jnp.bfloat16)


def attend_all(n_heads, head_dim, meta_ref, q_ref, kv_ref, o_ref, unit_out):
    n_blocks, n_batch, t_loc, _ = kv_ref.shape
    k_len = n_blocks * t_loc
    exponent = math.log2(math.e) / math.sqrt(head_dim)

    @pl.loop(0, n_batch)
    def _(b):
        at = pl.multiple_of(b * t_loc, t_loc)
        q = jnp.concatenate([q_ref[pl.ds(at, t_loc), i * head_dim:(i + 1) * head_dim] for i in range(n_heads)], axis=0)
        k = kv_ref[:, b, :, :head_dim].reshape(k_len, head_dim)
        v = kv_ref[:, b, :, head_dim:].reshape(k_len, head_dim)
        s = lax.dot_general(q, k, (((1,), (1,)), ((), ())), preferred_element_type=jnp.float32)
        q_pos = meta_ref[n_batch] + lax.broadcasted_iota(jnp.int32, (t_loc, 1), 0)
        k_pos = lax.broadcasted_iota(jnp.int32, (t_loc, k_len), 1)
        allowed = k_pos <= jnp.minimum(q_pos, meta_ref[b] - 1)
        s = jnp.where(jnp.concatenate([allowed] * n_heads, axis=0), s, NEG_BIG)
        e = jnp.exp2((s - jnp.max(s, axis=-1, keepdims=True)) * exponent)
        p = (e * (1.0 / jnp.sum(e, axis=-1, keepdims=True))).astype(jnp.bfloat16)
        o = jnp.dot(p, v, preferred_element_type=jnp.float32).astype(jnp.bfloat16)
        for i in range(n_heads):
            o_ref[0, pl.ds(at, t_loc), i * unit_out:i * unit_out + head_dim] = o[i * t_loc:(i + 1) * t_loc]


def gate_all(n_heads, head_dim, ff_head, skip, h_ref, w_ref, o_ref):
    unit_in = skip + 2 * ff_head
    unit_out = head_dim + ff_head
    tiles = ff_head // FF_TILE

    @pl.loop(0, n_heads * tiles)
    def _(step):
        head = step // tiles
        tile = step % tiles
        g_at = pl.multiple_of(head * unit_in + skip + tile * FF_TILE, 128)
        u_at = pl.multiple_of(head * unit_in + skip + ff_head + tile * FF_TILE, 128)
        m_at = pl.multiple_of(head * unit_out + head_dim + tile * FF_TILE, 128)
        gate = jnp.dot(h_ref[...], w_ref[0, :, pl.ds(g_at, FF_TILE)], preferred_element_type=jnp.float32)
        up = jnp.dot(h_ref[...], w_ref[0, :, pl.ds(u_at, FF_TILE)], preferred_element_type=jnp.float32)
        gate = gate.astype(jnp.bfloat16).astype(jnp.float32)
        up = up.astype(jnp.bfloat16).astype(jnp.float32)
        o_ref[0, :, pl.ds(m_at, FF_TILE)] = (gate * jax.nn.sigmoid(gate) * up).astype(jnp.bfloat16)


def heads_kernel(n_heads, head_dim, ff_head, meta_ref, h_ref, kv_ref, w_ref, o_ref, q_ref):
    unit_in = head_dim + 2 * ff_head
    w_q = jnp.concatenate([w_ref[0, :, i * unit_in:i * unit_in + head_dim] for i in range(n_heads)], axis=1)
    q_ref[...] = jnp.dot(h_ref[...], w_q, preferred_element_type=jnp.float32).astype(jnp.bfloat16)
    gate_all(n_heads, head_dim, ff_head, head_dim, h_ref, w_ref, o_ref)
    attend_all(n_heads, head_dim, meta_ref, q_ref, kv_ref, o_ref, head_dim + ff_head)


def attend_kernel(n_heads, head_dim, meta_ref, h_ref, kv_ref, w_ref, o_ref, q_ref):
    _, n_data, _, feat = w_ref.shape
    width = n_heads * head_dim
    w_q = jnp.concatenate([w_ref[0, y, :, i:i + width] for y in range(n_data) for i in range(0, feat, width)], axis=0)
    q_ref[...] = jnp.dot(h_ref[...], w_q, preferred_element_type=jnp.float32).astype(jnp.bfloat16)
    attend_all(n_heads, head_dim, meta_ref, q_ref, kv_ref, o_ref, head_dim)


def gate_kernel(n_heads, head_dim, ff_head, h_ref, a_ref, w_ref, o_ref):
    unit_out = head_dim + ff_head
    for i in range(n_heads):
        o_ref[0, :, i * unit_out:i * unit_out + head_dim] = a_ref[0, :, i * head_dim:(i + 1) * head_dim]
    gate_all(n_heads, head_dim, ff_head, 0, h_ref, w_ref, o_ref)


def out_kernel(at, x_ref, a_ref, w_ref, y_ref, acc_ref):
    group = pl.program_id(1)
    _, per, _, width = w_ref.shape
    feat = x_ref.shape[1] // per

    @pl.when(group == 0)
    def _():
        acc_ref[...] = jnp.zeros_like(acc_ref)

    w = jnp.concatenate([w_ref[0, c] for c in range(per)], axis=1)
    z = jnp.dot(a_ref[0], w, preferred_element_type=jnp.float32)
    acc_ref[...] += z.astype(jnp.bfloat16).astype(jnp.float32)

    @pl.when(group == pl.num_programs(1) - 1)
    def _():
        if width < feat:
            y_ref[...] = x_ref[...]
        for c in range(per):
            here = slice(c * feat + at, c * feat + at + width)
            y_ref[:, here] = (x_ref[:, here].astype(jnp.float32) + acc_ref[:, c * width:(c + 1) * width]).astype(jnp.bfloat16)


def group_call(kernel, args, specs, rows, out_cols, n_groups, flops, scratch=()):
    return pl.pallas_call(
        kernel,
        grid=(n_groups,),
        in_specs=specs,
        out_specs=pl.BlockSpec((1, rows, out_cols), lambda g: (g, 0, 0)),
        out_shape=jax.ShapeDtypeStruct((n_groups, rows, out_cols), jnp.bfloat16),
        scratch_shapes=list(scratch),
        compiler_params=pltpu.CompilerParams(vmem_limit_bytes=VMEM_LIMIT, dimension_semantics=("arbitrary",)),
        cost_estimate=pl.CostEstimate(flops=flops, bytes_accessed=2 * args[-1].size, transcendentals=0),
    )(*args)


def whole(arr):
    zeros = (0,) * arr.ndim
    return pl.BlockSpec(arr.shape, lambda g: zeros, pipeline_mode=pl.Buffered(1))


def project_heads(meta, h, kv, w_in, n_heads, head_dim, ff_head):
    n_groups, d_model, in_loc = w_in.shape
    rows = h.shape[0]
    return group_call(
        functools.partial(heads_kernel, n_heads, head_dim, ff_head),
        (meta, h, kv, w_in),
        [pl.BlockSpec(memory_space=pltpu.SMEM), whole(h), whole(kv), pl.BlockSpec((1, d_model, in_loc), lambda g: (g, 0, 0))],
        rows, n_heads * (head_dim + ff_head), n_groups, 2 * rows * d_model * in_loc * n_groups,
        [pltpu.VMEM((rows, n_heads * head_dim), jnp.bfloat16)],
    )


def attend_heads(meta, h, kv, w_packed, n_heads, head_dim):
    n_groups, n_data, packed_rows, feat = w_packed.shape
    rows, d_model = h.shape
    width = n_heads * head_dim
    q_rows = feat * width // feat
    last = packed_rows // q_rows - 1
    return group_call(
        functools.partial(attend_kernel, n_heads, head_dim),
        (meta, h, kv, w_packed),
        [pl.BlockSpec(memory_space=pltpu.SMEM), whole(h), whole(kv), pl.BlockSpec((1, n_data, q_rows, feat), lambda g: (g, 0, last, 0))],
        rows, width, n_groups, 2 * rows * d_model * width * n_groups,
        [pltpu.VMEM((rows, width), jnp.bfloat16)],
    )


def gate_heads(h, attended, w_gu, n_heads, head_dim, ff_head):
    n_groups, d_model, cols = w_gu.shape
    rows = h.shape[0]
    return group_call(
        functools.partial(gate_kernel, n_heads, head_dim, ff_head),
        (h, attended, w_gu),
        [whole(h), pl.BlockSpec((1, rows, n_heads * head_dim), lambda g: (g, 0, 0)), pl.BlockSpec((1, d_model, cols), lambda g: (g, 0, 0))],
        rows, n_heads * (head_dim + ff_head), n_groups, 2 * rows * d_model * cols * n_groups,
    )


def pack_queries(w_q):
    feat, width = w_q.shape
    return jnp.concatenate([w_q[i:i + width] for i in range(0, feat, width)], axis=1)


def project_out(x, joined, w_out, at):
    n_groups, n_data, _, width = w_out.shape
    out_loc = joined.shape[2]
    rows, d_model = x.shape
    feat = d_model // n_data
    per = n_data if n_data * width <= 2 * feat else 2
    return pl.pallas_call(
        functools.partial(out_kernel, at),
        grid=(n_data // per, n_groups),
        in_specs=[
            pl.BlockSpec((rows, per * feat), lambda c, g: (0, c)),
            pl.BlockSpec((1, rows, out_loc), lambda c, g: (g, 0, 0)),
            pl.BlockSpec((1, per, out_loc, width), lambda c, g: (g, c, 0, 0)),
        ],
        out_specs=pl.BlockSpec((rows, per * feat), lambda c, g: (0, c)),
        out_shape=jax.ShapeDtypeStruct((rows, d_model), jnp.bfloat16),
        scratch_shapes=[pltpu.VMEM((rows, per * width), jnp.float32)],
        compiler_params=pltpu.CompilerParams(vmem_limit_bytes=VMEM_LIMIT, dimension_semantics=("arbitrary", "arbitrary")),
        cost_estimate=pl.CostEstimate(flops=2 * rows * n_data * width * out_loc * n_groups, bytes_accessed=2 * w_out.size, transcendentals=0),
        name="project_out",
    )(x, joined, w_out)


def stack_by_shift(arr, axis, size, stride):
    n = size // stride

    def shift(value, r):
        return lax.ppermute(value, axis, [(i, (i + r * stride) % size) for i in range(size)])

    if n != 4:
        return jnp.stack([arr] + [shift(arr, r) for r in range(1, n)])
    back, ahead = shift(arr, 1), shift(arr, -1)
    half = arr.shape[0] // 2
    across = jnp.concatenate([shift(back[:half], 1), shift(ahead[half:], -1)])
    return jnp.stack([arr, back, across, ahead])


def absolute_order(rel, mine, n):
    return jnp.concatenate([lax.dynamic_slice_in_dim(rel, lax.rem(mine - i + n, n), 1, 0) for i in range(n)])


def swap_pair(value, n_model):
    other = lax.ppermute(value, "model", [(i, i ^ 1) for i in range(n_model)])
    first = lax.rem(lax.axis_index("model"), 2) == 0
    return jnp.where(first, value, other), jnp.where(first, other, value)


def gather_model(arr, n_model):
    mine = stack_by_shift(arr, "model", n_model, 2)
    both = jnp.stack(swap_pair(mine, n_model), axis=1)
    both = absolute_order(both, lax.axis_index("model") // 2, n_model // 2)
    return both.reshape((n_model,) + arr.shape)


def gather_kv_weights(w_kv, n_data, n_model):
    n_layers, feat, cols = w_kv.shape
    first = lax.rem(lax.axis_index("model"), 2) == 0
    half = jnp.where(first, w_kv[..., :cols // 2], w_kv[..., cols // 2:])
    half = absolute_order(stack_by_shift(half, "data", n_data, 1), lax.axis_index("data"), n_data)
    whole = jnp.concatenate(swap_pair(half, n_model), axis=-1)
    return whole.transpose(1, 0, 2, 3).reshape(n_layers, n_data * feat, cols)


def solution(mesh):
    n_model = mesh.shape["model"]
    n_data = mesh.shape["data"]
    act_spec = P(None, ("part", "data"), "model", None)
    ring = ("model", "data")

    def gather(arr):
        return lax.all_gather(arr, ring, axis=0, tiled=True)

    def layers_fn(x_blk, len_blk, gain_blk, w_in_blk, w_kv_blk, w_out_blk):
        n_layers, feat, in_loc = w_in_blk.shape
        head_dim = w_kv_blk.shape[2] // 2
        out_loc = w_out_blk.shape[1]
        heads_loc = (out_loc - (in_loc - out_loc)) // head_dim
        ff_head = out_loc // heads_loc - head_dim
        n_micro, n_seqs, t_loc, d_model = x_blk.shape
        n_batch = n_micro * n_seqs
        rows = n_batch * t_loc
        q_offset = lax.axis_index("model") * t_loc
        meta = jnp.concatenate([len_blk.reshape(n_batch), q_offset[None]]).astype(jnp.int32)

        unit_in = in_loc // heads_loc
        weights = []
        for layer in range(n_layers):
            heads = [w_in_blk[layer, :, i * unit_in:(i + 1) * unit_in] for i in range(heads_loc)]
            piece = w_in_blk[layer] if layer == 0 else jnp.concatenate([w[:, head_dim:] for w in heads], axis=1)
            w_in = gather(piece).reshape(n_model, d_model, piece.shape[1])
            w_outs = []
            last = layer == n_layers - 1
            cuts = (0, feat * 3 // 4, feat) if last else (0, feat)
            for lo, hi in zip(cuts, cuts[1:]):
                piece = w_out_blk[layer, :, lo:hi]
                if not last:
                    after = [w_in_blk[layer + 1, :, j * unit_in:j * unit_in + head_dim] for j in range(heads_loc)]
                    piece = jnp.concatenate([piece, pack_queries(jnp.concatenate(after, axis=1))])
                w_out = gather(piece)
                w_outs.append((lo, w_out.reshape((n_model, n_data) + piece.shape)))
            weights.append((w_in, w_outs))

        gain = lax.all_gather(gain_blk, "data", axis=1, tiled=True)
        w_kv = gather_kv_weights(w_kv_blk, n_data, n_model)

        hidden = x_blk.reshape(rows, d_model)
        for layer, (w_in, w_outs) in enumerate(weights):
            h = layer_norm(hidden, gain[layer])
            kv = jnp.dot(h, w_kv[layer], preferred_element_type=jnp.float32).astype(jnp.bfloat16)
            kv = gather_model(kv.reshape(n_batch, t_loc, 2 * head_dim), n_model)
            if layer == 0:
                joined = project_heads(meta, h, kv, w_in, heads_loc, head_dim, ff_head)
            else:
                attended = attend_heads(meta, h, kv, weights[layer - 1][1][-1][1], heads_loc, head_dim)
                joined = gate_heads(h, attended, w_in, heads_loc, head_dim, ff_head)
            for at, w_out in w_outs:
                hidden = project_out(hidden, joined, w_out, at)
        return hidden.reshape(x_blk.shape)

    return jax.shard_map(
        layers_fn,
        mesh=mesh,
        in_specs=(act_spec, P(None, ("part", "data")), P(None, "data"), P(None, "data", "model"), P(None, "data", None), P(None, "model", "data")),
        out_specs=act_spec,
        check_vma=False,
    )
```

time: 848 us -> 792 us (0.934)
  waiting for transfers between devices: 370 us -> 284 us
  Pallas kernels: 396 us -> 410 us
  blocking collectives: 0 us -> 9.66 us
    ppermute x11 -> x15, waiting for transfers between devices: 137 us -> 75.6 us  [the longest x12 70.1 us: shift(): lax.ppermute(value, axis, [(i, (i + r * stride) % size) for i in range(si...]
    all_gather x4 -> x5, waiting for transfers between devices: 232 us -> 208 us  [gather(): return lax.all_gather(arr, ring, axis=0, tiled=True)]
    pallas_call x4 -> x6, Pallas kernels: 396 us -> 410 us  [the longest x3 293 us: group_call(): pl.pallas_call(kernel, grid=(n_groups,), in_specs=specs, out_specs=pl.Blo...]
    all_gather x0 -> x1, blocking collectives: none -> 9.66 us  [layers_fn(): gain = lax.all_gather(gain_blk, 'data', axis=1, tiled=True)]
    ppermute x11 -> x15, starting transfers between devices: 25.9 us -> 29.1 us  [the longest x12 20.4 us: shift(): lax.ppermute(value, axis, [(i, (i + r * stride) % size) for i in range(si...]
  transfers between devices with their start and end apart: 15 -> 20, of which waited for: 11 -> 14; matrix products, arithmetic and copies ran while one was open for 4% -> 5% of each run, Pallas kernels for 41% -> 49%
where the time goes in v3:
time: 792 us
  Pallas kernels  410 us (52%)
  waiting for transfers between devices  284 us (36%)
  starting transfers between devices  29.4 us (4%)
  other arithmetic  28.9 us (4%)
  local copies, waits for them, and re-layouts  13.8 us (2%)
  between operations  13.7 us (2%)
  blocking collectives  9.66 us (1%)
    pallas_call x3, Pallas kernels, group_call(): pl.pallas_call(kernel, grid=(n_groups,), in_specs=specs, out_specs=pl.Blo...  293 us
    all_gather x5, waiting for transfers between devices, gather(): return lax.all_gather(arr, ring, axis=0, tiled=True)  208 us
    pallas_call x3, Pallas kernels, project_out(): pl.pallas_call(functools.partial(out_kernel, at), grid=(n_data // per, n_...  117 us
    ppermute x12, waiting for transfers between devices, shift(): lax.ppermute(value, axis, [(i, (i + r * stride) % size) for i in range(si...  70.1 us
    ppermute x12, starting transfers between devices, shift(): lax.ppermute(value, axis, [(i, (i + r * stride) % size) for i in range(si...  20.4 us
  transfers between devices with their start and end apart: 20, of which 14 were waited for; matrix products, arithmetic and copies ran while one was open for 5% of the time, Pallas kernels for 49%

profile of v3, /device:TPU:97, one launch (start us, length us, event | category | flops | bytes accessed | tf_op | source)
XLA Modules:
  0.0 792.2 jit_solution(16967624284755629452)
XLA Ops:
  6.6 3.4 slice.82
  12.6 1.8 slice_bitcast_fusion.2
  17.7 2.7 collective-permute-start
  20.4 2.6 collective-permute-start.2
  23.1 3.3 convert_reduce_fusion.1
  27.7 9.7 %all_gather.18 = bf16[2,2048]{1,0:T(2,128)(2,1)S(1)} all-gather(bf16[2,512]{1,0:T(2,128)(2,1)S(1)} %copy-done.6), channel_id=1, replica_groups=mesh['part'=1,'data'=4,'model'=8] {'data'}, dimensions={1}, use_global_device_ids=true | all-gather | bytes 10240 | tf_op jit(solution)/shard_map/all_gather | solution.py:273
  40.3 5.6 collective-permute-done.1
  46.7 5.6 collective-permute-start.4
  57.8 2.0 collective-permute-start.7
  59.7 16.9 %collective-permute-done.5 = bf16[8,128,256]{2,1,0:T(8,128)(2,1)S(1)} collective-permute-done((bf16[8,128,256]{2,1,0:T(8,128)(2,1)S(1)}, bf16[8,128,256]{2,1,0:T(8,128)(2,1)S(1)}, u32[]{:S(2)}, u32[]{:S(2)}) %collective-permute-start.5) | collective-permute-done | bytes 524320 | tf_op jit(solution)/shard_map/ppermute | solution.py:198
  76.8 2.9 collective-permute-start.8
  79.7 10.6 %collective-permute-done.6 = bf16[4,128,256]{2,1,0:T(8,128)(2,1)S(1)} collective-permute-done((bf16[4,128,256]{2,1,0:T(8,128)(2,1)S(1)}, bf16[4,128,256]{2,1,0:T(8,128)(2,1)S(1)}, u32[]{:S(2)}, u32[]{:S(2)}) %collective-permute-start.6) | collective-permute-done | bytes 262176 | tf_op jit(solution)/shard_map/ppermute | solution.py:198
  94.3 1.8 slice.97
  97.0 4.4 multiply_convert_fusion.h_ref
  104.1 2.3 copy.7
  106.5 134.8 %all-gather.13.cloned.1.call-done = bf16[1,16384,2304]{2,1,0:T(8,128)(2,1)} async-done(((bf16[1,512,2304]{2,1,0:T(8,128)(2,1)}), bf16[1,16384,2304]{2,1,0:T(8,128)(2,1)}) %all-gather.13.cloned.1.call-update) | async-done | bytes 75497488 | tf_op jit(solution)/shard_map/all_gather | solution.py:241
  241.2 144.5 %shard_map.64.a_ref = bf16[8,1024,1280]{2,1,0:T(8,128)(2,1)} custom-call(s32[9]{0:T(128)} %pad_add_fusion.meta_ref, bf16[1024,2048]{1,0:T(8,128)(2,1)} %multiply_convert_fusion.h_ref, bf16[8,8,128,256]{3,2,1,0:T(8,128)(2,1)} %bitcast.68, bf16[8,2048,2304]{2,1,0:T(8,128)(2,1)} %bitcast.20.w_ref), custom_call_target="tpu_custom_call" | custom-call | flops 77309411328 | bytes 75497472 | tf_op jit(solution)/shard_map/pallas_call | solution.py:111
  385.7 9.1 %all-gather.9.cloned.1.call-done = bf16[49152,512]{1,0:T(8,128)(2,1)} async-done(((bf16[1536,512]{1,0:T(8,128)(2,1)}), bf16[49152,512]{1,0:T(8,128)(2,1)}) %all-gather.9.cloned.1.call-update) | async-done | bytes 50331664 | tf_op jit(solution)/shard_map/all_gather | solution.py:241
  394.7 53.0 %project_out.3.x_ref = bf16[1024,2048]{1,0:T(8,128)(2,1)} custom-call(bf16[1024,2048]{1,0:T(8,128)(2,1)} %bitcast.62, bf16[8,1024,1280]{2,1,0:T(8,128)(2,1)} %shard_map.64.a_ref, bf16[8,4,1536,512]{3,2,1,0:T(8,128)(2,1)} %bitcast.63), custom_call_target="tpu_custom_call" | custom-call | flops 42949672960 | bytes 50331648 | tf_op jit(solution)/shard_map/project_out/pallas_call | solution.py:177
  447.8 3.7 convert_reduce_fusion
  460.0 23.8 %collective-permute-done.10 = bf16[8,128,256]{2,1,0:T(8,128)(2,1)S(1)} collective-permute-done((bf16[8,128,256]{2,1,0:T(8,128)(2,1)S(1)}, bf16[8,128,256]{2,1,0:T(8,128)(2,1)S(1)}, u32[]{:S(2)}, u32[]{:S(2)}) %collective-permute-start.10) | collective-permute-done | bytes 524320 | tf_op jit(solution)/shard_map/ppermute | solution.py:198
  483.9 2.9 collective-permute-start.13
  486.9 12.0 %collective-permute-done.11 = bf16[4,128,256]{2,1,0:T(8,128)(2,1)S(1)} collective-permute-done((bf16[4,128,256]{2,1,0:T(8,128)(2,1)S(1)}, bf16[4,128,256]{2,1,0:T(8,128)(2,1)S(1)}, u32[]{:S(2)}, u32[]{:S(2)}) %collective-permute-start.11) | collective-permute-done | bytes 262176 | tf_op jit(solution)/shard_map/ppermute | solution.py:198
  500.8 4.7 collective-permute-done.14
  506.3 2.3 pad_maximum_fusion.1
  508.6 66.0 %shard_map.65.a_ref = bf16[8,1024,256]{2,1,0:T(8,128)(2,1)} custom-call(s32[9]{0:T(128)} %pad_add_fusion.meta_ref, bf16[1024,2048]{1,0:T(8,128)(2,1)} %copy-done.3, bf16[8,8,128,256]{3,2,1,0:T(8,128)(2,1)} %bitcast.65, bf16[8,4,1536,512]{3,2,1,0:T(8,128)(2,1)} %bitcast.64), custom_call_target="tpu_custom_call" | custom-call | flops 8589934592 | bytes 50331648 | tf_op jit(solution)/shard_map/pallas_call | solution.py:111
  574.7 32.4 %all-gather.11.cloned.1.call-done = bf16[16384,2048]{1,0:T(8,128)(2,1)} async-done(((bf16[512,2048]{1,0:T(8,128)(2,1)}), bf16[16384,2048]{1,0:T(8,128)(2,1)}) %all-gather.11.cloned.1.call-update) | async-done | bytes 67108880 | tf_op jit(solution)/shard_map/all_gather | solution.py:241
  607.1 82.9 %shard_map.66.a_ref = bf16[8,1024,1280]{2,1,0:T(8,128)(2,1)} custom-call(bf16[1024,2048]{1,0:T(8,128)(2,1)} %copy-done.3, bf16[8,1024,256]{2,1,0:T(8,128)(2,1)} %shard_map.65.a_ref, bf16[8,2048,2048]{2,1,0:T(8,128)(2,1)} %bitcast.38.w_ref), custom_call_target="tpu_custom_call" | custom-call | flops 68719476736 | bytes 67108864 | tf_op jit(solution)/shard_map/pallas_call | solution.py:111
  690.0 21.3 %all-gather.15.cloned.1.call-done = bf16[1,40960,384]{2,1,0:T(8,128)(2,1)} async-done(((bf16[1,1280,384]{2,1,0:T(8,128)(2,1)}), bf16[1,40960,384]{2,1,0:T(8,128)(2,1)}) %all-gather.15.cloned.1.call-update) | async-done | bytes 31457296 | tf_op jit(solution)/shard_map/all_gather | solution.py:241
  711.3 43.5 %project_out.4.x_ref = bf16[1024,2048]{1,0:T(8,128)(2,1)} custom-call(bf16[1024,2048]{1,0:T(8,128)(2,1)} %project_out.3.x_ref, bf16[8,1024,1280]{2,1,0:T(8,128)(2,1)} %shard_map.66.a_ref, bf16[8,4,1280,384]{3,2,1,0:T(8,128)(2,1)} %bitcast.94), custom_call_target="tpu_custom_call" | custom-call | flops 32212254720 | bytes 31457280 | tf_op jit(solution)/shard_map/project_out/pallas_call | solution.py:177
  754.7 10.4 %all-gather.17.cloned.1.call-done = bf16[1,40960,128]{2,1,0:T(8,128)(2,1)} async-done(((bf16[1,1280,128]{2,1,0:T(8,128)(2,1)}), bf16[1,40960,128]{2,1,0:T(8,128)(2,1)}) %all-gather.17.cloned.1.call-update) | async-done | bytes 10485776 | tf_op jit(solution)/shard_map/all_gather | solution.py:241
  765.1 20.6 %project_out.5 = bf16[1024,2048]{1,0:T(8,128)(2,1)} custom-call(bf16[1024,2048]{1,0:T(8,128)(2,1)} %project_out.4.x_ref, bf16[8,1024,1280]{2,1,0:T(8,128)(2,1)} %shard_map.66.a_ref, bf16[8,4,1280,128]{3,2,1,0:T(8,128)(2,1)} %bitcast.66), custom_call_target="tpu_custom_call" | custom-call | flops 10737418240 | bytes 10485760 | tf_op jit(solution)/shard_map/project_out/pallas_call | solution.py:177
  (89 shorter events, 35.2 us)
Async XLA Ops:
  6.5 4.6 copy-start.4
  6.5 234.7 %all-gather.13.cloned.1.call-start = ((), (), s32[]{:S(2)}) async-start(), calls=%async_computation.2 | async-start | bytes 77856768 | tf_op jit(solution)/shard_map/all_gather | solution.py:241
  10.0 384.7 %all-gather.9.cloned.1.call-start = ((), (), s32[]{:S(2)}) async-start(), calls=%async_computation | async-start | bytes 51904512 | tf_op jit(solution)/shard_map/all_gather | solution.py:241
  12.6 594.5 %all-gather.11.cloned.1.call-start = ((), (), s32[]{:S(2)}) async-start(), calls=%async_computation.1 | async-start | bytes 69206016 | tf_op jit(solution)/shard_map/all_gather | solution.py:241
  14.7 2.9 copy-start.5
  16.3 694.9 %all-gather.15.cloned.1.call-start = ((), (), s32[]{:S(2)}) async-start(), calls=%async_computation.3 | async-start | bytes 32440320 | tf_op jit(solution)/shard_map/all_gather | solution.py:241
  17.5 747.5 %all-gather.17.cloned.1.call-start = ((), (), s32[]{:S(2)}) async-start(), calls=%async_computation.4 | async-start | bytes 10813440 | tf_op jit(solution)/shard_map/all_gather | solution.py:241
  17.6 8.8 %copy-start = (bf16[2,4,128,2048]{3,2,1,0:T(8,128)(2,1)S(1)}, bf16[2,4,128,2048]{3,2,1,0:T(8,128)(2,1)}, u32[]{:S(2)}) copy-start(bf16[2,4,128,2048]{3,2,1,0:T(8,128)(2,1)} %param.6) | copy-start | bytes 12582916
  17.7 10.0 %copy-start.6 = (bf16[2,512]{1,0:T(2,128)(2,1)S(1)}, bf16[2,512]{1,0:T(2,128)(2,1)}, u32[]{:S(2)}) copy-start(bf16[2,512]{1,0:T(2,128)(2,1)} %param.8) | copy-start | bytes 6148
  17.7 19.7 %collective-permute-start = (bf16[2,512,128]{2,1,0:T(8,128)(2,1)S(1)}, bf16[2,512,128]{2,1,0:T(8,128)(2,1)S(1)}, u32[]{:S(2)}, u32[]{:S(2)}) collective-permute-start(bf16[2,512,128]{2,1,0:T(8,128)(2,1)S(1)} %slice_select_fusion), channel_id=1, source_target_pairs={{0,8},{8,16},{16,24},{24,0},{1,9},{9,17},{17,25},{25,1},{2,10},{10... | collective-permute-start | bytes 786440 | tf_op jit(solution)/shard_map/ppermute | solution.py:198
  20.4 18.6 %collective-permute-start.2 = (bf16[2,512,128]{2,1,0:T(8,128)(2,1)S(1)}, bf16[2,512,128]{2,1,0:T(8,128)(2,1)S(1)}, u32[]{:S(2)}, u32[]{:S(2)}) collective-permute-start(bf16[2,512,128]{2,1,0:T(8,128)(2,1)S(1)} %slice_select_fusion), channel_id=1, source_target_pairs={{0,24},{8,0},{16,8},{24,16},{1,25},{9,1},{17,9},{25,17},{2,26},{10... | collective-permute-start | bytes 786440 | tf_op jit(solution)/shard_map/ppermute | solution.py:198
  27.7 24.6 %copy-start.1 = (bf16[2,4,128,2048]{3,2,1,0:T(8,128)(2,1)S(1)}, bf16[2,4,128,2048]{3,2,1,0:T(8,128)(2,1)}, u32[]{:S(2)}) copy-start(bf16[2,4,128,2048]{3,2,1,0:T(8,128)(2,1)} %param.6) | copy-start | bytes 12582916
  37.4 8.5 %collective-permute-start.1 = (bf16[1,512,128]{2,1,0:T(8,128)(2,1)S(1)}, bf16[1,512,128]{2,1,0:T(8,128)(2,1)S(1)}, u32[]{:S(2)}, u32[]{:S(2)}) collective-permute-start(bf16[1,512,128]{2,1,0:T(8,128)(2,1)S(1)} %slice.99), channel_id=1, source_target_pairs={{0,8},{8,16},{16,24},{24,0},{1,9},{9,17},{17,25},{25,1},{2,10},{10... | collective-permute-start | bytes 393224 | tf_op jit(solution)/shard_map/ppermute | solution.py:198
  39.0 7.2 collective-permute-start.3
  46.7 7.9 collective-permute-start.4
  56.4 39.9 %copy-start.7 = (s32[2,4]{1,0:T(2,128)S(1)}, s32[2,4]{1,0:T(2,128)}, u32[]{:S(2)}) copy-start(s32[2,4]{1,0:T(2,128)} %param.7) | copy-start | bytes 100
  56.4 20.2 %collective-permute-start.5 = (bf16[8,128,256]{2,1,0:T(8,128)(2,1)S(1)}, bf16[8,128,256]{2,1,0:T(8,128)(2,1)S(1)}, u32[]{:S(2)}, u32[]{:S(2)}) collective-permute-start(bf16[8,128,256]{2,1,0:T(8,128)(2,1)S(1)} %bitcast.77), channel_id=1, source_target_pairs={{0,2},{1,3},{2,4},{3,5},{4,6},{5,7},{6,0},{7,1},{8,10},{9,11},{10,... | collective-permute-start | bytes 1572872 | tf_op jit(solution)/shard_map/ppermute | solution.py:198
  57.8 19.0 %collective-permute-start.7 = (bf16[8,128,256]{2,1,0:T(8,128)(2,1)S(1)}, bf16[8,128,256]{2,1,0:T(8,128)(2,1)S(1)}, u32[]{:S(2)}, u32[]{:S(2)}) collective-permute-start(bf16[8,128,256]{2,1,0:T(8,128)(2,1)S(1)} %bitcast.78), channel_id=1, source_target_pairs={{0,6},{1,7},{2,0},{3,1},{4,2},{5,3},{6,4},{7,5},{8,14},{9,15},{10,... | collective-permute-start | bytes 1572872 | tf_op jit(solution)/shard_map/ppermute | solution.py:198
  76.6 13.6 %collective-permute-start.6 = (bf16[4,128,256]{2,1,0:T(8,128)(2,1)S(1)}, bf16[4,128,256]{2,1,0:T(8,128)(2,1)S(1)}, u32[]{:S(2)}, u32[]{:S(2)}) collective-permute-start(bf16[4,128,256]{2,1,0:T(8,128)(2,1)S(1)} %slice.102), channel_id=1, source_target_pairs={{0,2},{1,3},{2,4},{3,5},{4,6},{5,7},{6,0},{7,1},{8,10},{9,11},{10,... | collective-permute-start | bytes 786440 | tf_op jit(solution)/shard_map/ppermute | solution.py:198
  76.8 14.4 %collective-permute-start.8 = (bf16[4,128,256]{2,1,0:T(8,128)(2,1)S(1)}, bf16[4,128,256]{2,1,0:T(8,128)(2,1)S(1)}, u32[]{:S(2)}, u32[]{:S(2)}) collective-permute-start(bf16[4,128,256]{2,1,0:T(8,128)(2,1)S(1)} %slice.103), channel_id=1, source_target_pairs={{0,6},{1,7},{2,0},{3,1},{4,2},{5,3},{6,4},{7,5},{8,14},{9,15},{10,... | collective-permute-start | bytes 786440 | tf_op jit(solution)/shard_map/ppermute | solution.py:198
  92.8 8.5 %collective-permute-start.9 = (bf16[4,8,128,256]{3,2,1,0:T(8,128)(2,1)}, bf16[4,8,128,256]{3,2,1,0:T(8,128)(2,1)}, u32[]{:S(2)}, u32[]{:S(2)}) collective-permute-start(bf16[4,8,128,256]{3,2,1,0:T(8,128)(2,1)} %pad_maximum_fusion.2), channel_id=1, source_target_pairs={{0,1},{1,0},{2,3},{3,2},{4,5},{5,4},{6,7},{7,6},{8,9},{9,8},{10,11... | collective-permute-start | bytes 6291464 | tf_op jit(solution)/shard_map/ppermute | solution.py:213
  447.8 5.3 copy-start.2
  456.0 28.0 %copy-start.3 = (bf16[1024,2048]{1,0:T(8,128)(2,1)}, bf16[1024,2048]{1,0:T(8,128)(2,1)S(1)}, u32[]{:S(2)}) copy-start(bf16[1024,2048]{1,0:T(8,128)(2,1)S(1)} %fusion.6.h_ref) | copy-start | bytes 12582916
  457.2 26.5 %collective-permute-start.10 = (bf16[8,128,256]{2,1,0:T(8,128)(2,1)S(1)}, bf16[8,128,256]{2,1,0:T(8,128)(2,1)S(1)}, u32[]{:S(2)}, u32[]{:S(2)}) collective-permute-start(bf16[8,128,256]{2,1,0:T(8,128)(2,1)S(1)} %bitcast.81), channel_id=1, source_target_pairs={{0,2},{1,3},{2,4},{3,5},{4,6},{5,7},{6,0},{7,1},{8,10},{9,11},{10,... | collective-permute-start | bytes 1572872 | tf_op jit(solution)/shard_map/ppermute | solution.py:198
  458.2 25.7 %collective-permute-start.12 = (bf16[8,128,256]{2,1,0:T(8,128)(2,1)S(1)}, bf16[8,128,256]{2,1,0:T(8,128)(2,1)S(1)}, u32[]{:S(2)}, u32[]{:S(2)}) collective-permute-start(bf16[8,128,256]{2,1,0:T(8,128)(2,1)S(1)} %bitcast.82), channel_id=1, source_target_pairs={{0,6},{1,7},{2,0},{3,1},{4,2},{5,3},{6,4},{7,5},{8,14},{9,15},{10,... | collective-permute-start | bytes 1572872 | tf_op jit(solution)/shard_map/ppermute | solution.py:198
  483.8 15.1 %collective-permute-start.11 = (bf16[4,128,256]{2,1,0:T(8,128)(2,1)S(1)}, bf16[4,128,256]{2,1,0:T(8,128)(2,1)S(1)}, u32[]{:S(2)}, u32[]{:S(2)}) collective-permute-start(bf16[4,128,256]{2,1,0:T(8,128)(2,1)S(1)} %slice.108), channel_id=1, source_target_pairs={{0,2},{1,3},{2,4},{3,5},{4,6},{5,7},{6,0},{7,1},{8,10},{9,11},{10,... | collective-permute-start | bytes 786440 | tf_op jit(solution)/shard_map/ppermute | solution.py:198
  483.9 14.9 %collective-permute-start.13 = (bf16[4,128,256]{2,1,0:T(8,128)(2,1)S(1)}, bf16[4,128,256]{2,1,0:T(8,128)(2,1)S(1)}, u32[]{:S(2)}, u32[]{:S(2)}) collective-permute-start(bf16[4,128,256]{2,1,0:T(8,128)(2,1)S(1)} %slice.109), channel_id=1, source_target_pairs={{0,6},{1,7},{2,0},{3,1},{4,2},{5,3},{6,4},{7,5},{8,14},{9,15},{10,... | collective-permute-start | bytes 786440 | tf_op jit(solution)/shard_map/ppermute | solution.py:198
  499.2 6.3 collective-permute-start.14
Sparse Core Ops, SparseCore 0:
  10.1 231.0 all-gather.12
  243.3 151.3 all-gather.8
  396.8 210.2 all-gather.10
  609.1 102.1 all-gather.14
  713.2 51.8 all-gather.16

commit v4 on v3

--- a/solution.py
+++ b/solution.py
@@ -105,6 +105,64 @@
         for c in range(per):
             here = slice(c * feat + at, c * feat + at + width)
             y_ref[:, here] = (x_ref[:, here].astype(jnp.float32) + acc_ref[:, c * width:(c + 1) * width]).astype(jnp.bfloat16)
+
+
+def tail_kernel(at, x_ref, a_ref, w_ref, y_ref, part_ref, acc_ref, in_sem, out_sem):
+    group = pl.program_id(0)
+    _, per, _, width = w_ref.shape
+    feat = x_ref.shape[1] // per
+
+    def copy_in(c):
+        return pltpu.make_async_copy(x_ref.at[:, pl.ds(c * feat + at, width)], part_ref.at[:, pl.ds(c * width, width)], in_sem.at[c])
+
+    def copy_out(c):
+        return pltpu.make_async_copy(part_ref.at[:, pl.ds(c * width, width)], y_ref.at[:, pl.ds(c * feat + at, width)], out_sem.at[c])
+
+    @pl.when(group == 0)
+    def _():
+        for c in range(per):
+            copy_in(c).start()
+        acc_ref[...] = jnp.zeros_like(acc_ref)
+
+    w = jnp.concatenate([w_ref[0, c] for c in range(per)], axis=1)
+    z = jnp.dot(a_ref[0], w, preferred_element_type=jnp.float32)
+    acc_ref[...] += z.astype(jnp.bfloat16).astype(jnp.float32)
+
+    @pl.when(group == pl.num_programs(0) - 1)
+    def _():
+        for c in range(per):
+            copy_in(c).wait()
+        part_ref[...] = (part_ref[...].astype(jnp.float32) + acc_ref[...]).astype(jnp.bfloat16)
+        for c in range(per):
+            copy_out(c).start()
+        for c in range(per):
+            copy_out(c).wait()
+
+
+def project_tail(x, joined, w_out, at):
+    n_groups, n_data, out_loc, width = w_out.shape
+    rows, d_model = x.shape
+    return pl.pallas_call(
+        functools.partial(tail_kernel, at),
+        grid=(n_groups,),
+        in_specs=[
+            pl.BlockSpec(memory_space=pl.ANY),
+            pl.BlockSpec((1, rows, out_loc), lambda g: (g, 0, 0)),
+            pl.BlockSpec((1, n_data, out_loc, width), lambda g: (g, 0, 0, 0)),
+        ],
+        out_specs=pl.BlockSpec(memory_space=pl.ANY),
+        out_shape=jax.ShapeDtypeStruct((rows, d_model), jnp.bfloat16),
+        scratch_shapes=[
+            pltpu.VMEM((rows, n_data * width), jnp.bfloat16),
+            pltpu.VMEM((rows, n_data * width), jnp.float32),
+            pltpu.SemaphoreType.DMA((n_data,)),
+            pltpu.SemaphoreType.DMA((n_data,)),
+        ],
+        input_output_aliases={0: 0},
+        compiler_params=pltpu.CompilerParams(vmem_limit_bytes=VMEM_LIMIT, dimension_semantics=("arbitrary",)),
+        cost_estimate=pl.CostEstimate(flops=2 * rows * n_data * width * out_loc * n_groups, bytes_accessed=2 * w_out.size, transcendentals=0),
+        name="project_tail",
+    )(x, joined, w_out)
 
 
 def group_call(kernel, args, specs, rows, out_cols, n_groups, flops, scratch=()):
@@ -284,7 +342,8 @@
                 attended = attend_heads(meta, h, kv, weights[layer - 1][1][-1][1], heads_loc, head_dim)
                 joined = gate_heads(h, attended, w_in, heads_loc, head_dim, ff_head)
             for at, w_out in w_outs:
-                hidden = project_out(hidden, joined, w_out, at)
+                out = project_out if at == 0 else project_tail
+                hidden = out(hidden, joined, w_out, at)
         return hidden.reshape(x_blk.shape)
 
     return jax.shard_map(

time: 792 us -> 790 us (level)
    pallas_call x3 -> x2, Pallas kernels: 117 us -> 96.5 us  [project_out(): pl.pallas_call(functools.partial(out_kernel, at), grid=(n_data // per, n_...]
    pallas_call x0 -> x1, Pallas kernels: none -> 17.7 us  [project_tail(): pl.pallas_call(functools.partial(tail_kernel, at), grid=(n_groups,), in_s...]
where the time goes in v4:
time: 790 us; the launch traced here: 789 us
  Pallas kernels  408 us (52%)
  waiting for transfers between devices  284 us (36%)
  starting transfers between devices  29.4 us (4%)
  other arithmetic  29.1 us (4%)
  local copies, waits for them, and re-layouts  13.8 us (2%)
  between operations  13.7 us (2%)
  blocking collectives  9.66 us (1%)
    pallas_call x3, Pallas kernels, group_call(): pl.pallas_call(kernel, grid=(n_groups,), in_specs=specs, out_specs=pl.Blo...  293 us
    all_gather x5, waiting for transfers between devices, gather(): return lax.all_gather(arr, ring, axis=0, tiled=True)  208 us
    pallas_call x2, Pallas kernels, project_out(): pl.pallas_call(functools.partial(out_kernel, at), grid=(n_data // per, n_...  96.5 us
    ppermute x12, waiting for transfers between devices, shift(): lax.ppermute(value, axis, [(i, (i + r * stride) % size) for i in range(si...  70.1 us
    ppermute x12, starting transfers between devices, shift(): lax.ppermute(value, axis, [(i, (i + r * stride) % size) for i in range(si...  20.4 us
    pallas_call x1, Pallas kernels, project_tail(): pl.pallas_call(functools.partial(tail_kernel, at), grid=(n_groups,), in_s...  17.7 us
  transfers between devices with their start and end apart: 20, of which 14 were waited for; matrix products, arithmetic and copies ran while one was open for 5% of the time, Pallas kernels for 49%

profile of v4, /device:TPU:97, one launch (start us, length us, event | category | flops | bytes accessed | tf_op | source)
XLA Modules:
  0.0 789.4 jit_solution(10868504708743228655)
XLA Ops:
  6.6 3.4 slice.82
  12.6 1.8 slice_bitcast_fusion.2
  17.7 2.7 collective-permute-start
  20.4 2.6 collective-permute-start.2
  23.1 3.3 convert_reduce_fusion.1
  27.7 9.7 %all_gather.18 = bf16[2,2048]{1,0:T(2,128)(2,1)S(1)} all-gather(bf16[2,512]{1,0:T(2,128)(2,1)S(1)} %copy-done.6), channel_id=1, replica_groups=mesh['part'=1,'data'=4,'model'=8] {'data'}, dimensions={1}, use_global_device_ids=true | all-gather | bytes 10240 | tf_op jit(solution)/shard_map/all_gather | solution.py:331
  40.3 5.6 collective-permute-done.1
  46.7 5.6 collective-permute-start.4
  57.8 2.0 collective-permute-start.7
  59.7 16.9 %collective-permute-done.5 = bf16[8,128,256]{2,1,0:T(8,128)(2,1)S(1)} collective-permute-done((bf16[8,128,256]{2,1,0:T(8,128)(2,1)S(1)}, bf16[8,128,256]{2,1,0:T(8,128)(2,1)S(1)}, u32[]{:S(2)}, u32[]{:S(2)}) %collective-permute-start.5) | collective-permute-done | bytes 524320 | tf_op jit(solution)/shard_map/ppermute | solution.py:256
  76.8 2.9 collective-permute-start.8
  79.7 10.6 %collective-permute-done.6 = bf16[4,128,256]{2,1,0:T(8,128)(2,1)S(1)} collective-permute-done((bf16[4,128,256]{2,1,0:T(8,128)(2,1)S(1)}, bf16[4,128,256]{2,1,0:T(8,128)(2,1)S(1)}, u32[]{:S(2)}, u32[]{:S(2)}) %collective-permute-start.6) | collective-permute-done | bytes 262176 | tf_op jit(solution)/shard_map/ppermute | solution.py:256
  94.3 1.8 slice.97
  97.0 4.4 multiply_convert_fusion.h_ref
  104.1 2.3 copy.8
  106.5 134.8 %all-gather.13.cloned.1.call-done = bf16[1,16384,2304]{2,1,0:T(8,128)(2,1)} async-done(((bf16[1,512,2304]{2,1,0:T(8,128)(2,1)}), bf16[1,16384,2304]{2,1,0:T(8,128)(2,1)}) %all-gather.13.cloned.1.call-update) | async-done | bytes 75497488 | tf_op jit(solution)/shard_map/all_gather | solution.py:299
  241.2 144.5 %shard_map.64.a_ref = bf16[8,1024,1280]{2,1,0:T(8,128)(2,1)} custom-call(s32[9]{0:T(128)} %pad_add_fusion.meta_ref, bf16[1024,2048]{1,0:T(8,128)(2,1)} %multiply_convert_fusion.h_ref, bf16[8,8,128,256]{3,2,1,0:T(8,128)(2,1)} %bitcast.68, bf16[8,2048,2304]{2,1,0:T(8,128)(2,1)} %bitcast.20.w_ref), custom_call_target="tpu_custom_call" | custom-call | flops 77309411328 | bytes 75497472 | tf_op jit(solution)/shard_map/pallas_call | solution.py:169
  385.7 9.1 %all-gather.9.cloned.1.call-done = bf16[49152,512]{1,0:T(8,128)(2,1)} async-done(((bf16[1536,512]{1,0:T(8,128)(2,1)}), bf16[49152,512]{1,0:T(8,128)(2,1)}) %all-gather.9.cloned.1.call-update) | async-done | bytes 50331664 | tf_op jit(solution)/shard_map/all_gather | solution.py:299
  394.7 53.1 %project_out.2.x_ref = bf16[1024,2048]{1,0:T(8,128)(2,1)} custom-call(bf16[1024,2048]{1,0:T(8,128)(2,1)} %bitcast.62, bf16[8,1024,1280]{2,1,0:T(8,128)(2,1)} %shard_map.64.a_ref, bf16[8,4,1536,512]{3,2,1,0:T(8,128)(2,1)} %bitcast.63), custom_call_target="tpu_custom_call" | custom-call | flops 42949672960 | bytes 50331648 | tf_op jit(solution)/shard_map/project_out/pallas_call | solution.py:235
  447.8 3.8 convert_reduce_fusion
  460.1 23.8 %collective-permute-done.10 = bf16[8,128,256]{2,1,0:T(8,128)(2,1)S(1)} collective-permute-done((bf16[8,128,256]{2,1,0:T(8,128)(2,1)S(1)}, bf16[8,128,256]{2,1,0:T(8,128)(2,1)S(1)}, u32[]{:S(2)}, u32[]{:S(2)}) %collective-permute-start.10) | collective-permute-done | bytes 524320 | tf_op jit(solution)/shard_map/ppermute | solution.py:256
  484.1 2.9 collective-permute-start.13
  487.0 12.0 %collective-permute-done.11 = bf16[4,128,256]{2,1,0:T(8,128)(2,1)S(1)} collective-permute-done((bf16[4,128,256]{2,1,0:T(8,128)(2,1)S(1)}, bf16[4,128,256]{2,1,0:T(8,128)(2,1)S(1)}, u32[]{:S(2)}, u32[]{:S(2)}) %collective-permute-start.11) | collective-permute-done | bytes 262176 | tf_op jit(solution)/shard_map/ppermute | solution.py:256
  500.9 4.8 collective-permute-done.14
  506.6 2.4 pad_maximum_fusion.1
  508.9 66.0 %shard_map.65.a_ref = bf16[8,1024,256]{2,1,0:T(8,128)(2,1)} custom-call(s32[9]{0:T(128)} %pad_add_fusion.meta_ref, bf16[1024,2048]{1,0:T(8,128)(2,1)} %copy-done.3, bf16[8,8,128,256]{3,2,1,0:T(8,128)(2,1)} %bitcast.65, bf16[8,4,1536,512]{3,2,1,0:T(8,128)(2,1)} %bitcast.64), custom_call_target="tpu_custom_call" | custom-call | flops 8589934592 | bytes 50331648 | tf_op jit(solution)/shard_map/pallas_call | solution.py:169
  575.0 32.1 %all-gather.11.cloned.1.call-done = bf16[16384,2048]{1,0:T(8,128)(2,1)} async-done(((bf16[512,2048]{1,0:T(8,128)(2,1)}), bf16[16384,2048]{1,0:T(8,128)(2,1)}) %all-gather.11.cloned.1.call-update) | async-done | bytes 67108880 | tf_op jit(solution)/shard_map/all_gather | solution.py:299
  607.1 82.9 %shard_map.66.a_ref = bf16[8,1024,1280]{2,1,0:T(8,128)(2,1)} custom-call(bf16[1024,2048]{1,0:T(8,128)(2,1)} %copy-done.3, bf16[8,1024,256]{2,1,0:T(8,128)(2,1)} %shard_map.65.a_ref, bf16[8,2048,2048]{2,1,0:T(8,128)(2,1)} %bitcast.38.w_ref), custom_call_target="tpu_custom_call" | custom-call | flops 68719476736 | bytes 67108864 | tf_op jit(solution)/shard_map/pallas_call | solution.py:169
  690.0 21.3 %all-gather.15.cloned.1.call-done = bf16[1,40960,384]{2,1,0:T(8,128)(2,1)} async-done(((bf16[1,1280,384]{2,1,0:T(8,128)(2,1)}), bf16[1,40960,384]{2,1,0:T(8,128)(2,1)}) %all-gather.15.cloned.1.call-update) | async-done | bytes 31457296 | tf_op jit(solution)/shard_map/all_gather | solution.py:299
  711.3 43.4 %project_out.3.x_ref = bf16[1024,2048]{1,0:T(8,128)(2,1)} custom-call(bf16[1024,2048]{1,0:T(8,128)(2,1)} %project_out.2.x_ref, bf16[8,1024,1280]{2,1,0:T(8,128)(2,1)} %shard_map.66.a_ref, bf16[8,4,1280,384]{3,2,1,0:T(8,128)(2,1)} %bitcast.94), custom_call_target="tpu_custom_call" | custom-call | flops 32212254720 | bytes 31457280 | tf_op jit(solution)/shard_map/project_out/pallas_call | solution.py:235
  754.7 10.4 %all-gather.17.cloned.1.call-done = bf16[1,40960,128]{2,1,0:T(8,128)(2,1)} async-done(((bf16[1,1280,128]{2,1,0:T(8,128)(2,1)}), bf16[1,40960,128]{2,1,0:T(8,128)(2,1)}) %all-gather.17.cloned.1.call-update) | async-done | bytes 10485776 | tf_op jit(solution)/shard_map/all_gather | solution.py:299
  765.1 17.7 %project_tail.1 = bf16[1024,2048]{1,0:T(8,128)(2,1)} custom-call(bf16[1024,2048]{1,0:T(8,128)(2,1)} %project_out.3.x_ref, bf16[8,1024,1280]{2,1,0:T(8,128)(2,1)} %shard_map.66.a_ref, bf16[8,4,1280,128]{3,2,1,0:T(8,128)(2,1)} %bitcast.66), custom_call_target="tpu_custom_call", output_to_operand_aliasing={{}: (0, {})} | custom-call | flops 10737418240 | bytes 10485760 | tf_op jit(solution)/shard_map/project_tail/pallas_call | solution.py:145
  (89 shorter events, 35.2 us)
Async XLA Ops:
  6.5 4.6 copy-start.4
  6.5 234.7 %all-gather.13.cloned.1.call-start = ((), (), s32[]{:S(2)}) async-start(), calls=%async_computation.2 | async-start | bytes 77856768 | tf_op jit(solution)/shard_map/all_gather | solution.py:299
  10.0 384.7 %all-gather.9.cloned.1.call-start = ((), (), s32[]{:S(2)}) async-start(), calls=%async_computation | async-start | bytes 51904512 | tf_op jit(solution)/shard_map/all_gather | solution.py:299
  12.6 594.5 %all-gather.11.cloned.1.call-start = ((), (), s32[]{:S(2)}) async-start(), calls=%async_computation.1 | async-start | bytes 69206016 | tf_op jit(solution)/shard_map/all_gather | solution.py:299
  14.7 2.9 copy-start.5
  16.3 694.9 %all-gather.15.cloned.1.call-start = ((), (), s32[]{:S(2)}) async-start(), calls=%async_computation.3 | async-start | bytes 32440320 | tf_op jit(solution)/shard_map/all_gather | solution.py:299
  17.5 747.6 %all-gather.17.cloned.1.call-start = ((), (), s32[]{:S(2)}) async-start(), calls=%async_computation.4 | async-start | bytes 10813440 | tf_op jit(solution)/shard_map/all_gather | solution.py:299
  17.6 8.8 %copy-start = (bf16[2,4,128,2048]{3,2,1,0:T(8,128)(2,1)S(1)}, bf16[2,4,128,2048]{3,2,1,0:T(8,128)(2,1)}, u32[]{:S(2)}) copy-start(bf16[2,4,128,2048]{3,2,1,0:T(8,128)(2,1)} %param.6) | copy-start | bytes 12582916
  17.7 10.0 %copy-start.6 = (bf16[2,512]{1,0:T(2,128)(2,1)S(1)}, bf16[2,512]{1,0:T(2,128)(2,1)}, u32[]{:S(2)}) copy-start(bf16[2,512]{1,0:T(2,128)(2,1)} %param.8) | copy-start | bytes 6148
  17.7 19.7 %collective-permute-start = (bf16[2,512,128]{2,1,0:T(8,128)(2,1)S(1)}, bf16[2,512,128]{2,1,0:T(8,128)(2,1)S(1)}, u32[]{:S(2)}, u32[]{:S(2)}) collective-permute-start(bf16[2,512,128]{2,1,0:T(8,128)(2,1)S(1)} %slice_select_fusion), channel_id=1, source_target_pairs={{0,8},{8,16},{16,24},{24,0},{1,9},{9,17},{17,25},{25,1},{2,10},{10... | collective-permute-start | bytes 786440 | tf_op jit(solution)/shard_map/ppermute | solution.py:256
  20.4 18.6 %collective-permute-start.2 = (bf16[2,512,128]{2,1,0:T(8,128)(2,1)S(1)}, bf16[2,512,128]{2,1,0:T(8,128)(2,1)S(1)}, u32[]{:S(2)}, u32[]{:S(2)}) collective-permute-start(bf16[2,512,128]{2,1,0:T(8,128)(2,1)S(1)} %slice_select_fusion), channel_id=1, source_target_pairs={{0,24},{8,0},{16,8},{24,16},{1,25},{9,1},{17,9},{25,17},{2,26},{10... | collective-permute-start | bytes 786440 | tf_op jit(solution)/shard_map/ppermute | solution.py:256
  27.7 24.6 %copy-start.1 = (bf16[2,4,128,2048]{3,2,1,0:T(8,128)(2,1)S(1)}, bf16[2,4,128,2048]{3,2,1,0:T(8,128)(2,1)}, u32[]{:S(2)}) copy-start(bf16[2,4,128,2048]{3,2,1,0:T(8,128)(2,1)} %param.6) | copy-start | bytes 12582916
  37.4 8.5 %collective-permute-start.1 = (bf16[1,512,128]{2,1,0:T(8,128)(2,1)S(1)}, bf16[1,512,128]{2,1,0:T(8,128)(2,1)S(1)}, u32[]{:S(2)}, u32[]{:S(2)}) collective-permute-start(bf16[1,512,128]{2,1,0:T(8,128)(2,1)S(1)} %slice.99), channel_id=1, source_target_pairs={{0,8},{8,16},{16,24},{24,0},{1,9},{9,17},{17,25},{25,1},{2,10},{10... | collective-permute-start | bytes 393224 | tf_op jit(solution)/shard_map/ppermute | solution.py:256
  39.0 7.2 collective-permute-start.3
  46.7 7.9 %collective-permute-start.4 = (bf16[4,2,512,128]{3,2,1,0:T(8,128)(2,1)S(1)}, bf16[4,2,512,128]{3,2,1,0:T(8,128)(2,1)S(1)}, u32[]{:S(2)}, u32[]{:S(2)}) collective-permute-start(bf16[4,2,512,128]{3,2,1,0:T(8,128)(2,1)S(1)} %pad_maximum_fusion.6), channel_id=1, source_target_pairs={{0,1},{1,0},{2,3},{3,2},{4,5},{5,4},{6,7},{7,6},{8,9},{9,8},{10,11... | collective-permute-start | bytes 3145736 | tf_op jit(solution)/shard_map/ppermute | solution.py:271
  56.4 39.9 %copy-start.7 = (s32[2,4]{1,0:T(2,128)S(1)}, s32[2,4]{1,0:T(2,128)}, u32[]{:S(2)}) copy-start(s32[2,4]{1,0:T(2,128)} %param.7) | copy-start | bytes 100
  56.4 20.2 %collective-permute-start.5 = (bf16[8,128,256]{2,1,0:T(8,128)(2,1)S(1)}, bf16[8,128,256]{2,1,0:T(8,128)(2,1)S(1)}, u32[]{:S(2)}, u32[]{:S(2)}) collective-permute-start(bf16[8,128,256]{2,1,0:T(8,128)(2,1)S(1)} %bitcast.77), channel_id=1, source_target_pairs={{0,2},{1,3},{2,4},{3,5},{4,6},{5,7},{6,0},{7,1},{8,10},{9,11},{10,... | collective-permute-start | bytes 1572872 | tf_op jit(solution)/shard_map/ppermute | solution.py:256
  57.8 19.0 %collective-permute-start.7 = (bf16[8,128,256]{2,1,0:T(8,128)(2,1)S(1)}, bf16[8,128,256]{2,1,0:T(8,128)(2,1)S(1)}, u32[]{:S(2)}, u32[]{:S(2)}) collective-permute-start(bf16[8,128,256]{2,1,0:T(8,128)(2,1)S(1)} %bitcast.78), channel_id=1, source_target_pairs={{0,6},{1,7},{2,0},{3,1},{4,2},{5,3},{6,4},{7,5},{8,14},{9,15},{10,... | collective-permute-start | bytes 1572872 | tf_op jit(solution)/shard_map/ppermute | solution.py:256
  76.6 13.6 %collective-permute-start.6 = (bf16[4,128,256]{2,1,0:T(8,128)(2,1)S(1)}, bf16[4,128,256]{2,1,0:T(8,128)(2,1)S(1)}, u32[]{:S(2)}, u32[]{:S(2)}) collective-permute-start(bf16[4,128,256]{2,1,0:T(8,128)(2,1)S(1)} %slice.102), channel_id=1, source_target_pairs={{0,2},{1,3},{2,4},{3,5},{4,6},{5,7},{6,0},{7,1},{8,10},{9,11},{10,... | collective-permute-start | bytes 786440 | tf_op jit(solution)/shard_map/ppermute | solution.py:256
  76.8 14.4 %collective-permute-start.8 = (bf16[4,128,256]{2,1,0:T(8,128)(2,1)S(1)}, bf16[4,128,256]{2,1,0:T(8,128)(2,1)S(1)}, u32[]{:S(2)}, u32[]{:S(2)}) collective-permute-start(bf16[4,128,256]{2,1,0:T(8,128)(2,1)S(1)} %slice.103), channel_id=1, source_target_pairs={{0,6},{1,7},{2,0},{3,1},{4,2},{5,3},{6,4},{7,5},{8,14},{9,15},{10,... | collective-permute-start | bytes 786440 | tf_op jit(solution)/shard_map/ppermute | solution.py:256
  92.8 8.5 %collective-permute-start.9 = (bf16[4,8,128,256]{3,2,1,0:T(8,128)(2,1)}, bf16[4,8,128,256]{3,2,1,0:T(8,128)(2,1)}, u32[]{:S(2)}, u32[]{:S(2)}) collective-permute-start(bf16[4,8,128,256]{3,2,1,0:T(8,128)(2,1)} %pad_maximum_fusion.2), channel_id=1, source_target_pairs={{0,1},{1,0},{2,3},{3,2},{4,5},{5,4},{6,7},{7,6},{8,9},{9,8},{10,11... | collective-permute-start | bytes 6291464 | tf_op jit(solution)/shard_map/ppermute | solution.py:271
  447.8 5.4 copy-start.2
  456.1 28.0 %copy-start.3 = (bf16[1024,2048]{1,0:T(8,128)(2,1)}, bf16[1024,2048]{1,0:T(8,128)(2,1)S(1)}, u32[]{:S(2)}) copy-start(bf16[1024,2048]{1,0:T(8,128)(2,1)S(1)} %fusion.6.h_ref) | copy-start | bytes 12582916
  457.4 26.5 %collective-permute-start.10 = (bf16[8,128,256]{2,1,0:T(8,128)(2,1)S(1)}, bf16[8,128,256]{2,1,0:T(8,128)(2,1)S(1)}, u32[]{:S(2)}, u32[]{:S(2)}) collective-permute-start(bf16[8,128,256]{2,1,0:T(8,128)(2,1)S(1)} %bitcast.81), channel_id=1, source_target_pairs={{0,2},{1,3},{2,4},{3,5},{4,6},{5,7},{6,0},{7,1},{8,10},{9,11},{10,... | collective-permute-start | bytes 1572872 | tf_op jit(solution)/shard_map/ppermute | solution.py:256
  458.3 25.7 %collective-permute-start.12 = (bf16[8,128,256]{2,1,0:T(8,128)(2,1)S(1)}, bf16[8,128,256]{2,1,0:T(8,128)(2,1)S(1)}, u32[]{:S(2)}, u32[]{:S(2)}) collective-permute-start(bf16[8,128,256]{2,1,0:T(8,128)(2,1)S(1)} %bitcast.82), channel_id=1, source_target_pairs={{0,6},{1,7},{2,0},{3,1},{4,2},{5,3},{6,4},{7,5},{8,14},{9,15},{10,... | collective-permute-start | bytes 1572872 | tf_op jit(solution)/shard_map/ppermute | solution.py:256
  483.9 15.1 %collective-permute-start.11 = (bf16[4,128,256]{2,1,0:T(8,128)(2,1)S(1)}, bf16[4,128,256]{2,1,0:T(8,128)(2,1)S(1)}, u32[]{:S(2)}, u32[]{:S(2)}) collective-permute-start(bf16[4,128,256]{2,1,0:T(8,128)(2,1)S(1)} %slice.108), channel_id=1, source_target_pairs={{0,2},{1,3},{2,4},{3,5},{4,6},{5,7},{6,0},{7,1},{8,10},{9,11},{10,... | collective-permute-start | bytes 786440 | tf_op jit(solution)/shard_map/ppermute | solution.py:256
  484.1 14.9 %collective-permute-start.13 = (bf16[4,128,256]{2,1,0:T(8,128)(2,1)S(1)}, bf16[4,128,256]{2,1,0:T(8,128)(2,1)S(1)}, u32[]{:S(2)}, u32[]{:S(2)}) collective-permute-start(bf16[4,128,256]{2,1,0:T(8,128)(2,1)S(1)} %slice.109), channel_id=1, source_target_pairs={{0,6},{1,7},{2,0},{3,1},{4,2},{5,3},{6,4},{7,5},{8,14},{9,15},{10,... | collective-permute-start | bytes 786440 | tf_op jit(solution)/shard_map/ppermute | solution.py:256
  499.3 6.4 collective-permute-start.14
Sparse Core Ops, SparseCore 0:
  10.1 231.0 all-gather.12
  243.3 151.3 all-gather.8
  396.8 210.2 all-gather.10
  609.1 102.1 all-gather.14
  713.2 51.8 all-gather.16
